TPU v7x, 32 devices: a whole 2x2x4 slice. The times are simulated.
32 devices in a mesh: fsdp: 32 (over z, y, x, core).
Axes of the slice: x: 2, y: 2, z: 4, core: 2. Of those that a mesh axis runs over, the one named last changes fastest.
Arguments:
- block_input: bfloat16 [12288, 1152], P('fsdp'), may hold values from -6 to 6
- params: bfloat16 [1, 15241216], P(None, 'fsdp'), may hold values from -4 to 4, as said below
- cotangent: bfloat16 [12288, 1152], P('fsdp'), may hold values from -6 to 6
- segment_ids: int32 [12288], replicated, may hold values from 0 to 17, never falling along the last dimension, each value on 1 to 729 neighbouring positions
Outputs:
- activations: bfloat16 [12288, 1152], P('fsdp')
- input_grad: bfloat16 [12288, 1152], P('fsdp')
- param_grads: float32 [1, 15241216], P(None, 'fsdp')
Inputs may be any that keep to these rules, and one draw needn't show every extreme that they name: `segment_ids`: image ids never fall along the tokens; each image holds 1 to 729 tokens, one exactly 729. `params`: gains lie around one, biases and weights around zero.
All inputs are finite; a program needn't handle non-finite values.
Results may differ from a plain program's by a relative error of at most 0.012.
Values may be sent and summed in bfloat16 or wider, within the bound.
A program may use at most 320 MiB of HBM per device.

v0:
```python
import functools
import math

import jax
import jax.numpy as jnp
import numpy as np
from jax import lax
from jax.experimental import pallas as pl
from jax.experimental.pallas import tpu as pltpu
from jax.sharding import PartitionSpec as P

D = 1152
HEADS = 16
HEAD_DIM = 72
FF = 4304
REACH = 2


EPS = 1e-06
NEG = -1e30
LANES = 128
ROWS = 16
DC = D // LANES
FC = -(-FF // LANES)
WIDE = FF * ROWS // LANES
HEAD = 544
KIND_A, KIND_D, KIND_L2, KIND_L3, KIND_B = 1, 2, 3, 4, 5
MESH = pl.DeviceIdType.MESH


def units():
    found = []
    offset = 0

    def matrix(name, kind, rows, width, tiles):
        nonlocal offset
        for row in range(0, rows, ROWS):
            found.append((name, kind, offset + row * width, tiles))
        offset += rows * width

    def vectors(name, kind, length, tiles):
        nonlocal offset
        found.append((name, kind, offset, tiles))
        offset += length

    vectors("vec1", KIND_L2, 2 * D, 2)
    matrix("w_query", KIND_A, D, D, DC)
    matrix("w_key", KIND_A, D, D, DC)
    matrix("w_value", KIND_A, D, D, DC)
    vectors("vec2", KIND_L2, 2 * D, 2)
    matrix("w_out", KIND_A, D, D, DC)
    vectors("vec3", KIND_L2, 3 * D, 2)
    matrix("w_up", KIND_B, D, FF, FC)
    vectors("vec4", KIND_L3, FF, 3)
    matrix("w_down", KIND_D, FF, D, DC)
    vectors("vec5", KIND_D, D, DC)
    return found


def unit_width(name):
    return {"vec1": 2 * D, "vec2": 2 * D, "vec3": 3 * D, "vec4": FF, "vec5": D, "w_up": ROWS * FF}.get(
        name, ROWS * D
    )


def wire_plan(count, shard):
    blocks = [[] for _ in range(count)]
    where = {}
    used = [0] * count
    tails = [0] * count
    for name, kind, first, tiles in units():
        owner = first // shard
        where.setdefault(name, []).append((owner, used[owner], tiles))
        blocks[owner].append((kind, (first - owner * shard) // LANES, used[owner]))
        used[owner] += tiles
        tails[owner] = max(0, first + unit_width(name) - (owner + 1) * shard)
    block = max(used)
    block += block % 2
    most = max(len(b) for b in blocks)
    table = np.zeros((count, 3 * most), np.int32)
    for owner, entries in enumerate(blocks):
        for i, entry in enumerate(entries):
            table[owner, 3 * i : 3 * i + 3] = entry
    return where, block, table, np.array(tails, np.int32)


def lane_iota(rows):
    return lax.broadcasted_iota(jnp.int32, (rows, LANES), 1)


def wide_rows():
    return [divmod(row * FF, LANES) for row in range(ROWS)]


SKEW = (D * 0 + 80) % LANES


def rows_from_line(line_ref, flat_ref, first, rows):
    step = 8 * LANES

    @pl.loop(0, rows // 8)
    def _(i):
        part = line_ref[:, pl.ds(pl.multiple_of(i * step, step), step)].astype(jnp.float32)
        flat_ref[pl.ds(first + i * 8, 8)] = part.reshape(8, LANES)

    for row in range(rows // 8 * 8, rows):
        flat_ref[pl.ds(first + row, 1)] = line_ref[:, row * LANES : (row + 1) * LANES].astype(jnp.float32)


def line_from_rows(flat_ref, line_ref, first, rows):
    step = 8 * LANES

    @pl.loop(0, rows // 8)
    def _(i):
        part = flat_ref[pl.ds(first + i * 8, 8)]
        line_ref[:, pl.ds(pl.multiple_of(i * step, step), step)] = part.reshape(1, step)

    for row in range(rows // 8 * 8, rows):
        line_ref[:, row * LANES : (row + 1) * LANES] = flat_ref[pl.ds(first + row, 1)]


def to_tiles_kernel(entries, table_ref, line_ref, head_ref, tile_ref, stage_ref, flat_ref):
    rows = line_ref.shape[1] // LANES
    rows_from_line(line_ref, flat_ref, 0, rows)
    rows_from_line(head_ref, flat_ref, rows, HEAD)

    def unit(i, _):
        kind, src, dst = (table_ref[3 * i + j] for j in range(3))

        @pl.when(kind == KIND_A)
        def _():
            for c in range(DC):
                tile_ref[dst + c] = flat_ref[pl.ds(src + c, ROWS, stride=DC), :].astype(jnp.bfloat16)

        @pl.when(kind == KIND_D)
        def _():
            lane = lane_iota(ROWS)
            for c in range(DC):
                here = flat_ref[pl.ds(src + c, ROWS, stride=DC), :]
                after = flat_ref[pl.ds(src + c + 1, ROWS, stride=DC), :]
                both = jnp.where(lane >= SKEW, here, after)
                tile_ref[dst + c] = pltpu.roll(both, LANES - SKEW, 1).astype(jnp.bfloat16)

        for code, tiles in ((KIND_L2, 2), (KIND_L3, 3)):

            @pl.when(kind == code)
            def _():
                for j in range(tiles):
                    tile_ref[dst + j] = flat_ref[pl.ds(src + ROWS * j, ROWS), :].astype(jnp.bfloat16)

        @pl.when(kind == KIND_B)
        def _():
            tall = 8 * pl.cdiv(FC, 8)
            lane = lane_iota(tall)
            row = lax.broadcasted_iota(jnp.int32, (tall, LANES), 0)
            keep = (row < FC - 1) | (lane < FF % LANES)
            for r, (base, skew) in enumerate(wide_rows()):
                part = flat_ref[pl.ds(src + base, tall), :]
                if skew:
                    after = flat_ref[pl.ds(src + base + 1, tall), :]
                    part = pltpu.roll(jnp.where(lane >= skew, part, after), LANES - skew, 1)
                stage_ref[pl.ds(r, tall, stride=ROWS), :] = jnp.where(keep, part, 0.0)
            for c in range(FC):
                tile_ref[dst + c] = stage_ref[pl.ds(ROWS * c, ROWS), :].astype(jnp.bfloat16)

        return 0

    lax.fori_loop(0, entries, unit, 0)


def to_flat_kernel(entries, rows, table_ref, tile_ref, *refs):
    if len(refs) == 5:
        tail_ref, line_ref, stage_ref, flat_ref, first_ref = refs
    else:
        line_ref, stage_ref, flat_ref = refs
    if len(refs) == 5:
        flat_ref[...] = jnp.zeros_like(flat_ref)

    def unit(i, _):
        kind, src, dst = (table_ref[3 * i + j] for j in range(3))

        @pl.when(kind == KIND_A)
        def _():
            for c in range(DC):
                flat_ref[pl.ds(src + c, ROWS, stride=DC), :] = tile_ref[dst + c]

        @pl.when(kind == KIND_D)
        def _():
            lane = lane_iota(ROWS)
            for c in range(DC):
                turned = pltpu.roll(tile_ref[dst + c], SKEW, 1)
                for step, keep in ((0, lane >= SKEW), (1, lane < SKEW)):
                    at = pl.ds(src + c + step, ROWS, stride=DC)
                    flat_ref[at, :] = jnp.where(keep, turned, flat_ref[at, :])

        for code, tiles in ((KIND_L2, 2), (KIND_L3, 3)):

            @pl.when(kind == code)
            def _():
                for j in range(tiles):
                    flat_ref[pl.ds(src + ROWS * j, ROWS), :] = tile_ref[dst + j]

        @pl.when(kind == KIND_B)
        def _():
            tall = 8 * pl.cdiv(FC, 8)
            lane = lane_iota(tall)
            row = lax.broadcasted_iota(jnp.int32, (tall, LANES), 0)
            for c in range(FC):
                stage_ref[pl.ds(ROWS * c, ROWS), :] = tile_ref[dst + c]
            for r, (base, skew) in enumerate(wide_rows()):
                turned = stage_ref[pl.ds(r, tall, stride=ROWS), :]
                if skew:
                    turned = pltpu.roll(turned, skew, 1)
                for step in range(2 if skew else 1):
                    entry = row * LANES + lane + (step * LANES - skew)
                    keep = (lane < skew if step else lane >= skew) & (entry < FF)
                    at = pl.ds(src + base + step, tall)
                    flat_ref[at, :] = jnp.where(keep, turned, flat_ref[at, :])

        return 0

    lax.fori_loop(0, entries, unit, 0)
    if len(refs) == 3:
        line_from_rows(flat_ref, line_ref, rows, HEAD)
        return
    rows_from_line(tail_ref, first_ref, 0, HEAD)
    entry = lax.broadcasted_iota(jnp.int32, (HEAD, LANES), 0) * LANES + lane_iota(HEAD)
    flat_ref[:HEAD] = jnp.where(entry < table_ref[3 * entries], first_ref[...], flat_ref[:HEAD])
    line_from_rows(flat_ref, line_ref, 0, rows)


def my_row(table):
    return lax.dynamic_index_in_dim(jnp.asarray(table), lax.axis_index("fsdp"), 0, keepdims=False)


def relayout_scratch(rows):
    return [
        pltpu.VMEM((ROWS * 8 * pl.cdiv(FC, 8), LANES), jnp.float32),
        pltpu.VMEM((8 * pl.cdiv(rows + HEAD + 8, 8), LANES), jnp.float32),
    ]


def to_tiles(line, plan):
    where, block, table, tails = plan
    count = lax.axis_size("fsdp")
    head = lax.ppermute(line[:, : HEAD * LANES], "fsdp", [(i, (i - 1) % count) for i in range(count)])
    vmem = pl.BlockSpec(memory_space=pltpu.VMEM)
    return pl.pallas_call(
        functools.partial(to_tiles_kernel, table.shape[1] // 3),
        out_shape=jax.ShapeDtypeStruct((block, ROWS, LANES), jnp.bfloat16),
        grid_spec=pltpu.PrefetchScalarGridSpec(
            num_scalar_prefetch=1, grid=(1,), in_specs=[vmem, vmem], out_specs=vmem,
            scratch_shapes=relayout_scratch(line.shape[1] // LANES),
        ),
        name="to_tiles",
    )(my_row(table), line, head)


def to_flat(tiles, plan, length):
    where, block, table, tails = plan
    count = lax.axis_size("fsdp")
    rows = length // LANES
    vmem = pl.BlockSpec(memory_space=pltpu.VMEM)
    last = [max(i for i in range(table.shape[1] // 3) if row[3 * i]) for row in table]
    last = np.stack([row[3 * i : 3 * i + 3] for row, i in zip(table, last)])
    whole = np.concatenate([table, np.roll(tails, 1)[:, None]], axis=1)

    def call(entries, mine, inputs, width, scratch, name):
        return pl.pallas_call(
            functools.partial(to_flat_kernel, entries, rows),
            out_shape=jax.ShapeDtypeStruct((1, width), jnp.float32),
            grid_spec=pltpu.PrefetchScalarGridSpec(
                num_scalar_prefetch=1, grid=(1,), in_specs=[vmem] * len(inputs), out_specs=vmem,
                scratch_shapes=relayout_scratch(rows) + scratch,
            ),
            name=name,
        )(my_row(mine), *inputs)

    tail = call(1, last, (tiles,), HEAD * LANES, [], "tail")
    tail = lax.ppermute(tail, "fsdp", [(i, (i + 1) % count) for i in range(count)])
    return call(table.shape[1] // 3, whole, (tiles, tail), length, [pltpu.VMEM((HEAD, LANES), jnp.float32)], "to_flat")


def place(me):
    return lax.rem(me, 2), lax.rem(me // 2, 2), lax.rem(me // 4, 2), me // 8


def index_of(core, x, y, z):
    return ((z * 2 + y) * 2 + x) * 2 + core


def greet(devices_and_conditions):
    barrier = pltpu.get_barrier_semaphore()
    for device, present in devices_and_conditions:
        if present is None:
            pl.semaphore_signal(barrier, inc=1, device_id=(device,), device_id_type=MESH)
        else:

            @pl.when(present)
            def _():
                pl.semaphore_signal(barrier, inc=1, device_id=(device,), device_id_type=MESH)

    present = [1 if p is None else p.astype(jnp.int32) for _, p in devices_and_conditions]
    pl.semaphore_wait(barrier, sum(present))


BF = jnp.bfloat16
F32 = jnp.float32
PAIR = 2 * LANES
SCALE = HEAD_DIM**-0.5
GELU_A = math.sqrt(2.0 / math.pi)
GELU_B = 0.044715
LOG2E = math.log2(math.e)
ANY = pl.BlockSpec(memory_space=pl.ANY)
VM = pl.BlockSpec(memory_space=pltpu.VMEM)
VMEM_LIMIT = 63 << 20


def nn(left, right):
    return lax.dot_general(left, right, (((1,), (0,)), ((), ())), preferred_element_type=F32)


def nt(left, right):
    return lax.dot_general(left, right, (((1,), (1,)), ((), ())), preferred_element_type=F32)


def runs_of(where, name):
    runs, done = [], 0
    for owner, at, tiles in where[name]:
        if runs and runs[-1][0] == owner and runs[-1][1] + runs[-1][2] == at:
            runs[-1][2] += tiles
        else:
            runs.append([owner, at, tiles, done])
        done += tiles
    return runs


def copies(where, name, blocks_ref, tiles_ref, sem, out=False):
    made = []
    flat_tiles = tiles_ref if len(tiles_ref.shape) == 3 else tiles_ref.reshape(-1, ROWS, LANES)
    for owner, at, tiles, done in runs_of(where, name):
        there, here = blocks_ref.at[owner, pl.ds(at, tiles)], flat_tiles.at[pl.ds(done, tiles)]
        made.append(pltpu.make_async_copy(here, there, sem) if out else pltpu.make_async_copy(there, here, sem))
    return made


def start(made):
    for copy in made:
        copy.start()


def wait(made):
    for copy in made:
        copy.wait()


def panel(tiles_ref, c, units, first=0):
    return tiles_ref[pl.ds(first, units), pl.ds(c, 1)].reshape(units * ROWS, LANES)


def panels(tiles_ref, c, many, units, first=0):
    return jnp.concatenate([panel(tiles_ref, c + i, units, first) for i in range(many)], axis=1)


def put_panel(tiles_ref, c, value, first=0):
    units = value.shape[0] // ROWS
    tiles_ref[pl.ds(first, units), pl.ds(c, 1)] = value.astype(BF).reshape(units, 1, ROWS, LANES)


def put_panels(tiles_ref, c, value, first=0):
    for i in range(value.shape[1] // LANES):
        put_panel(tiles_ref, c + i, value[:, i * LANES : (i + 1) * LANES], first)


def over_pairs(body):
    @pl.loop(0, DC // 2)
    def _(pair):
        body(2 * pair, 2)

    if DC % 2:
        body(DC - 1, 1)


def lanes_of(c, many):
    return pl.ds(c * LANES if isinstance(c, int) else pl.multiple_of(c * LANES, LANES), many * LANES)


def vector_rows(tiles_ref):
    return jnp.concatenate([tiles_ref[i].astype(F32) for i in range(tiles_ref.shape[0])], axis=0)


def as_row(rows, first, many):
    return jnp.concatenate([rows[first + i : first + i + 1] for i in range(many)], axis=1)


def put_vectors(tiles_ref, rows_list):
    parts = [row[:, i * LANES : (i + 1) * LANES] for row in rows_list for i in range(row.shape[1] // LANES)]
    missing = tiles_ref.shape[0] * ROWS - len(parts)
    whole = jnp.concatenate(parts + [jnp.zeros((missing, LANES), F32)] if missing else parts, axis=0)
    for i in range(tiles_ref.shape[0]):
        tiles_ref[i] = whole[i * ROWS : (i + 1) * ROWS].astype(BF)


def norm_rows(values):
    centre = values - jnp.mean(values, axis=-1, keepdims=True)
    inverse = lax.rsqrt(jnp.mean(centre * centre, axis=-1, keepdims=True) + EPS)
    return centre * inverse, inverse


def norm_rows_back(grad, normed, inverse, gain):
    scaled = grad * gain
    return inverse * (
        scaled - jnp.mean(scaled, axis=-1, keepdims=True) - normed * jnp.mean(scaled * normed, axis=-1, keepdims=True)
    )


def column_sums(values):
    return jnp.sum(values, axis=0, keepdims=True)


def head_window(h):
    block = jnp.minimum((h * HEAD_DIM) // LANES, DC - 2)
    lane = pl.multiple_of(block * LANES, LANES)
    return lane, h * HEAD_DIM - lane


def head_mask(rows, offset):
    lane = lax.broadcasted_iota(jnp.int32, (rows, PAIR), 1)
    return (lane >= offset) & (lane < offset + HEAD_DIM)


def front_kernel(
    where, x_ref, segq_ref, segk_ref, blocks_ref, q_ref, k_ref, v_ref, attended_ref, rest_ref, logs_ref,
    normed_ref, w_ref, vec1_ref, vec2_ref, bias_ref, score_ref, prob_ref, sem, vec_sem,
):
    window, rows = x_ref.shape[0], q_ref.shape[0]
    margin = (window - rows) // 2
    loads = [copies(where, name, blocks_ref, w_ref.at[i], sem.at[i]) for i, name in enumerate(("w_query", "w_key", "w_value"))]
    vecs = copies(where, "vec1", blocks_ref, vec1_ref, vec_sem) + copies(where, "vec2", blocks_ref, vec2_ref, vec_sem)
    start(vecs)
    for made in loads:
        start(made)
    wait(vecs)
    vec = vector_rows(vec1_ref)
    gain, shift = as_row(vec, 0, DC), as_row(vec, DC, DC)
    step = rows // 3

    @pl.loop(0, window // step)
    def _(i):
        at = pl.ds(i * step, step)
        normed, _ = norm_rows(x_ref[at].astype(F32))
        normed_ref[at] = (normed * gain + shift).astype(BF)

    @pl.loop(0, rows // 8)
    def _(i):
        at = pl.ds(i * 8, 8)
        bias_ref[at] = jnp.where(segq_ref[at] == segk_ref[...], 0.0, NEG)

    biases = vector_rows(vec2_ref)
    zero = jnp.zeros((1, D), F32)
    for made in loads:
        wait(made)
    for i, (out, add) in enumerate(((q_ref, as_row(biases, 0, DC)), (k_ref, zero), (v_ref, as_row(biases, DC, DC)))):
        for c in range(0, DC, 2):
            many = min(2, DC - c)
            lanes = slice(c * LANES, (c + many) * LANES)
            weights = panels(w_ref.at[i], c, many, D // ROWS)
            if i == 0:
                out[:, lanes] = (nn(normed_ref[pl.ds(margin, rows)], weights) + add[:, lanes]).astype(BF)
            else:

                @pl.loop(0, window // rows)
                def _(b):
                    at = pl.ds(b * rows, rows)
                    out[at, lanes] = (nn(normed_ref[at], weights) + add[:, lanes]).astype(BF)

    attended_ref[...] = jnp.zeros_like(attended_ref)
    rest_ref[...] = jnp.zeros_like(rest_ref)
    logs_ref[...] = jnp.zeros_like(logs_ref)
    lane_l = lax.broadcasted_iota(jnp.int32, logs_ref.shape, 1)

    @pl.loop(0, HEADS)
    def _(h):
        lane, offset = head_window(h)
        mask = head_mask(rows, offset)
        lanes = pl.ds(lane, PAIR)
        query = jnp.where(mask, q_ref[:, lanes], jnp.zeros((), BF))
        score_ref[...] = nt(query, k_ref[:, lanes]) * SCALE + bias_ref[...]
        top = jnp.max(score_ref[...], axis=-1, keepdims=True)
        powers = jnp.exp(score_ref[...] - top)
        total = jnp.sum(powers, axis=-1, keepdims=True)
        prob_ref[...] = powers.astype(BF)
        out = nn(prob_ref[...], v_ref[:, lanes]) / total
        rounded = out.astype(BF)
        attended_ref[:, lanes] = jnp.where(mask, rounded, attended_ref[:, lanes])
        rest_ref[:, lanes] = jnp.where(mask, (out - rounded.astype(F32)).astype(BF), rest_ref[:, lanes])
        logs_ref[...] = jnp.where(lane_l == h, top + jnp.log(total), logs_ref[...])


def front(x_win, seg_query, seg_keys, gathered, where, rows):
    window = x_win.shape[0]
    shape = lambda n, d=D, t=BF: jax.ShapeDtypeStruct((n, d), t)
    dma = pltpu.SemaphoreType.DMA
    units = D // ROWS
    return pl.pallas_call(
        functools.partial(front_kernel, where),
        out_shape=(shape(rows), shape(window), shape(window), shape(rows), shape(rows), shape(rows, LANES, F32)),
        in_specs=[VM, VM, VM, ANY],
        out_specs=[VM] * 6,
        scratch_shapes=[
            pltpu.VMEM((window, D), BF),
            pltpu.VMEM((3, units, DC, ROWS, LANES), BF), pltpu.VMEM((2, ROWS, LANES), BF), pltpu.VMEM((2, ROWS, LANES), BF),
            pltpu.VMEM((rows, window), F32), pltpu.VMEM((rows, window), F32), pltpu.VMEM((rows, window), BF), dma((3,)), dma,
        ],
        compiler_params=pltpu.CompilerParams(vmem_limit_bytes=VMEM_LIMIT),
        name="front",
    )(x_win, seg_query, seg_keys, gathered)


def middle_kernel(
    where, x_ref, cot_ref, attended_ref, rest_ref, blocks_ref, act_ref, mid_grad_ref, att_grad_ref, delta_ref, parts_ref,
    wo_ref, wu_ref, wd_ref, vec3_ref, vec4_ref, vec5_ref, b_up_ref, hidden_ref, slope_ref, pre_ref, normed_ref, normed_b_ref,
    mid_ref, g_up_ref, mid_b_ref, sem, out_sem,
):
    rows = x_ref.shape[0]
    units, f_units = D // ROWS, FF // ROWS
    names = ("w_out", "w_up", "w_down", "vec3", "vec4", "vec5")
    refs = (wo_ref, wu_ref, wd_ref, vec3_ref, vec4_ref, vec5_ref)
    loads = {n: copies(where, n, blocks_ref, r, sem.at[i]) for i, (n, r) in enumerate(zip(names, refs))}
    saves = {n: copies(where, n, parts_ref, r, out_sem, out=True) for n, r in zip(names, refs)}
    for n in ("vec3", "vec4", "vec5", "w_out", "w_up", "w_down"):
        start(loads[n])
    f_wide = FC * LANES
    pads = f_wide // ROWS - f_units
    wd_ref[pl.ds(f_units, pads)] = jnp.zeros((pads, DC, ROWS, LANES), BF)
    for n in ("vec3", "vec4", "vec5", "w_out"):
        wait(loads[n])
    vec = vector_rows(vec3_ref)
    b_out, gain, shift = (as_row(vec, i * DC, DC) for i in range(3))
    vec = vector_rows(vec4_ref)
    entry = lax.broadcasted_iota(jnp.int32, vec.shape, 0) * LANES + lax.broadcasted_iota(jnp.int32, vec.shape, 1)
    b_up_ref[...] = jnp.where(entry < FF, vec, 0.0)
    b_down = jnp.concatenate([vec5_ref[c].astype(F32)[0:1] for c in range(DC)], axis=1)

    for c in range(0, DC, 2):
        many = min(2, DC - c)
        lanes = slice(c * LANES, (c + many) * LANES)
        mid_ref[:, lanes] = (
            x_ref[:, lanes].astype(F32) + nn(attended_ref[...], panels(wo_ref, c, many, units)) + b_out[:, lanes]
        )
    normed, inverse = norm_rows(mid_ref[...])
    normed_ref[...] = normed
    normed_b_ref[...] = (normed * gain + shift).astype(BF)

    wait(loads["w_up"])

    @pl.loop(0, FC // 2)
    def _(p):
        at = pl.ds(pl.multiple_of(p * PAIR, PAIR), PAIR)
        bias = jnp.concatenate([b_up_ref[pl.ds(2 * p, 1)], b_up_ref[pl.ds(2 * p + 1, 1)]], axis=1)
        v = nn(normed_b_ref[...], panels(wu_ref, 2 * p, 2, units)) + bias
        square = v * v
        bent = jnp.tanh(GELU_A * v * (1.0 + GELU_B * square))
        hidden_ref[:, at] = (0.5 * v * (1.0 + bent)).astype(BF)
        slope_ref[:, at] = 0.5 * (1.0 + bent) + 0.5 * v * (1.0 - bent * bent) * (
            GELU_A * (1.0 + 3.0 * GELU_B * square)
        )

    wait(loads["w_down"])
    for c in range(0, DC, 2):
        many = min(2, DC - c)
        lanes = slice(c * LANES, (c + many) * LANES)
        act_ref[:, lanes] = (
            mid_ref[:, lanes] + nn(hidden_ref[...], panels(wd_ref, c, many, f_wide // ROWS)) + b_down[:, lanes]
        ).astype(BF)

    @pl.loop(0, FC // 2)
    def _(p):
        at = pl.ds(pl.multiple_of(p * PAIR, PAIR), PAIR)
        first = p * (PAIR // ROWS)
        grad = nt(cot_ref[...], panels(wd_ref, 0, DC, PAIR // ROWS, first)) * slope_ref[:, at]
        pre_ref[:, at] = grad.astype(BF)
        sums = column_sums(grad)
        g_up_ref[pl.ds(2 * p, 1)] = sums[:, :LANES]
        g_up_ref[pl.ds(2 * p + 1, 1)] = sums[:, LANES:]
        put_panels(wd_ref, 0, nn(hidden_ref[:, at].T, cot_ref[...]), first)

    start(saves["w_down"])
    put_vectors(vec4_ref, [b_up_row for b_up_row in [g_up_ref[i : i + 1] for i in range(FC)]])
    start(saves["vec4"])
    cot = cot_ref[...].astype(F32)
    sums = column_sums(cot)
    row0 = lax.broadcasted_iota(jnp.int32, (ROWS, LANES), 0) == 0
    for c in range(DC):
        vec5_ref[c] = jnp.where(row0, sums[:, c * LANES : (c + 1) * LANES], 0.0).astype(BF)
    start(saves["vec5"])

    for c in range(0, DC, 2):
        many = min(2, DC - c)
        weights = panels(wu_ref, 0, FC, many * LANES // ROWS, c * LANES // ROWS)
        mid_ref[:, c * LANES : (c + many) * LANES] = nt(pre_ref[...], weights)
    turned_b = normed_b_ref[...].T

    @pl.loop(0, FC // 2)
    def _(p):
        at = pl.ds(pl.multiple_of(p * PAIR, PAIR), PAIR)
        put_panels(wu_ref, 2 * p, nn(turned_b, pre_ref[:, at]))

    start(saves["w_up"])
    e = mid_ref[...]
    normed = normed_ref[...]
    g_gain, g_shift = column_sums(e * normed), column_sums(e)
    mid_grad = cot + norm_rows_back(e, normed, inverse, gain)
    mid_grad_ref[...] = mid_grad
    put_vectors(vec3_ref, [column_sums(mid_grad), g_gain, g_shift])
    start(saves["vec3"])
    mid_b = mid_grad.astype(BF)
    mid_b_ref[...] = mid_b

    def attended_grad(c, many):
        weights = panels(wo_ref, 0, DC, many * LANES // ROWS, c * (LANES // ROWS))
        att_grad_ref[:, lanes_of(c, many)] = nt(mid_b_ref[...], weights).astype(BF)

    over_pairs(attended_grad)
    product = att_grad_ref[...].astype(F32) * (attended_ref[...].astype(F32) + rest_ref[...].astype(F32))
    delta_ref[...] = jnp.sum(product.T.reshape(HEADS, HEAD_DIM, rows), axis=1)
    turned = attended_ref[...].T
    over_pairs(lambda c, many: put_panels(wo_ref, c, nn(turned, mid_b_ref[:, lanes_of(c, many)])))
    start(saves["w_out"])
    for n in names:
        wait(saves[n])


def middle(block_input, cotangent, attended, rest, gathered, where):
    rows = block_input.shape[0]
    shape = lambda t: jax.ShapeDtypeStruct((rows, D), t)
    dma = pltpu.SemaphoreType.DMA
    tiles = lambda *n: pltpu.VMEM((*n, ROWS, LANES), BF)
    units, f_wide = D // ROWS, FC * LANES
    return pl.pallas_call(
        functools.partial(middle_kernel, where),
        out_shape=(shape(BF), shape(F32), shape(BF), jax.ShapeDtypeStruct((HEADS, rows), F32), jax.ShapeDtypeStruct(gathered.shape, BF)),
        in_specs=[VM, VM, VM, VM, ANY],
        out_specs=[VM, VM, VM, VM, ANY],
        scratch_shapes=[
            tiles(units, DC), tiles(units, FC), tiles(f_wide // ROWS, DC), tiles(2), tiles(3), tiles(DC),
            pltpu.VMEM((3 * ROWS, LANES), F32), pltpu.VMEM((rows, f_wide), BF), pltpu.VMEM((rows, f_wide), F32),
            pltpu.VMEM((rows, f_wide), BF), pltpu.VMEM((rows, D), F32), pltpu.VMEM((rows, D), BF), pltpu.VMEM((rows, D), F32),
            pltpu.VMEM((3 * ROWS, LANES), F32), pltpu.VMEM((rows, D), BF), dma((6,)), dma,
        ],
        compiler_params=pltpu.CompilerParams(vmem_limit_bytes=VMEM_LIMIT),
        name="middle",
    )(block_input, cotangent, attended, rest, gathered)


def back_kernel(
    where, x_hbm_ref, segq_ref, segk_ref, blocks_ref, q_ref, k_ref, v_ref, grad_ref, logs_ref, parts_in_ref,
    near_ref, own_ref, parts_ref,
    w_ref, vec1_ref, vec2_ref, bias_ref, score_ref, prob_ref, turned_ref, dk_ref, dv_ref, dq_ref, part_ref, logs_t_ref, x_ref,
    sem, vec_sem, out_sem, x_sem,
):
    window, rows = x_ref.shape[0], q_ref.shape[0]
    margin = (window - rows) // 2
    units = D // ROWS
    names = ("w_query", "w_key", "w_value")
    loads = [copies(where, name, blocks_ref, w_ref.at[i], sem.at[i]) for i, name in enumerate(names)]
    vecs = copies(where, "vec1", blocks_ref, vec1_ref, vec_sem)
    start(vecs)
    for made in loads:
        start(made)
    x_load = pltpu.make_async_copy(x_hbm_ref, x_ref, x_sem)
    x_load.start()

    @pl.loop(0, window // LANES)
    def _(i):
        at = pl.ds(pl.multiple_of(i * LANES, LANES), LANES)
        bias_ref[at] = jnp.where(segk_ref[at] == segq_ref[...], 0.0, NEG)
        turned_ref[:, at] = k_ref[at].T
        dk_ref[at] = jnp.zeros((LANES, D), F32)
        dv_ref[at] = jnp.zeros((LANES, D), F32)

    logs_t_ref[...] = logs_ref[...].T

    @pl.loop(0, HEADS)
    def _(h):
        lane, offset = head_window(h)
        mask = head_mask(rows, offset)
        lanes = pl.ds(lane, PAIR)
        query = jnp.where(mask, q_ref[:, lanes], jnp.zeros((), BF))
        grad = jnp.where(mask, grad_ref[:, lanes], jnp.zeros((), BF))
        probs = jnp.exp(nt(k_ref[:, lanes], query) * SCALE + bias_ref[...] - logs_t_ref[pl.ds(h, 1)])
        score_ref[...] = probs
        prob_ref[...] = probs.astype(BF)
        prob_grad = nt(v_ref[:, lanes], grad)
        row_total = jnp.sum(score_ref[...] * prob_grad, axis=0, keepdims=True)
        dv_ref[:, lanes] += nn(prob_ref[...], grad)
        prob_ref[...] = (score_ref[...] * (prob_grad - row_total)).astype(BF)
        dk_ref[:, lanes] += nn(prob_ref[...], query)
        part_ref[...] = nn(turned_ref[lanes], prob_ref[...])
        at = pl.ds(pl.multiple_of(h * HEAD_DIM, 8), HEAD_DIM)
        dq_ref[at] = part_ref[pl.ds(pl.multiple_of(offset, 8), HEAD_DIM)]

    dq = dq_ref[...].T * SCALE
    g_query = column_sums(dq)
    dq_b = dq.astype(BF)
    wait(vecs)
    vec = vector_rows(vec1_ref)
    gain, shift = as_row(vec, 0, DC), as_row(vec, DC, DC)
    dk_b_ref, dv_b_ref = k_ref, v_ref
    x_load.wait()
    g_value = jnp.zeros((1, D), F32)
    step = rows // 3

    def rounded(i, total):
        at = pl.ds(pl.multiple_of(i * step, step), step)
        dk_b_ref[at] = (dk_ref[at] * SCALE).astype(BF)
        dv = dv_ref[at]
        dv_b_ref[at] = dv.astype(BF)
        normed, _ = norm_rows(x_ref[at].astype(F32))
        turned_ref[:, at] = (normed * gain + shift).astype(BF).T
        return total + column_sums(dv)

    g_value = lax.fori_loop(0, window // step, rounded, g_value)
    put_vectors(vec2_ref, [g_query, g_value])
    save = copies(where, "vec2", parts_ref, vec2_ref, out_sem, out=True)
    for made in loads:
        wait(made)
    for c in range(0, DC, 2):
        many = min(2, DC - c)
        lanes = slice(c * LANES, (c + many) * LANES)
        part = [panels(w_ref.at[i], 0, DC, many * LANES // ROWS, c * LANES // ROWS) for i in range(3)]

        @pl.loop(0, window // rows)
        def _(b):
            at = pl.ds(b * rows, rows)
            dk_ref[at, lanes] = nt(dk_b_ref[at], part[1]) + nt(dv_b_ref[at], part[2])

        dk_ref[pl.ds(margin, rows), lanes] += nt(dq_b, part[0])
    turned_own = turned_ref[:, pl.ds(margin, rows)]
    for c in range(0, DC, 2):
        many = min(2, DC - c)
        lanes = slice(c * LANES, (c + many) * LANES)
        put_panels(w_ref.at[0], c, nn(turned_own, dq_b[:, lanes]))
        put_panels(w_ref.at[1], c, nn(turned_ref[...], dk_b_ref[:, lanes]))
        put_panels(w_ref.at[2], c, nn(turned_ref[...], dv_b_ref[:, lanes]))
    for i, name in enumerate(names):
        save = save + copies(where, name, parts_ref, w_ref.at[i], out_sem, out=True)
    start(save)

    def norm_block(i, totals):
        at = pl.ds(pl.multiple_of(i * step, step), step)
        normed, inverse = norm_rows(x_ref[at].astype(F32))
        e = dk_ref[at]
        part = norm_rows_back(e, normed, inverse, gain)
        x_ref[at] = part.astype(BF)

        @pl.when((i >= margin // step) & (i < (margin + rows) // step))
        def _():
            own_ref[pl.ds(pl.multiple_of(i * step - margin, step), step)] = part

        return totals[0] + column_sums(e * normed), totals[1] + column_sums(e)

    zero = jnp.zeros((1, D), F32)
    g_gain, g_shift = lax.fori_loop(0, window // step, norm_block, (zero, zero))
    put_vectors(vec1_ref, [g_gain, g_shift])
    last = copies(where, "vec1", parts_ref, vec1_ref, out_sem, out=True)
    last = last + [pltpu.make_async_copy(x_ref, near_ref, x_sem)]
    start(last)
    wait(save + last)


def back(x_win, seg_query, seg_keys, gathered, queries, key_win, value_win, att_grad, logs, parts, where):
    window, rows = x_win.shape[0], queries.shape[0]
    dma = pltpu.SemaphoreType.DMA
    tiles = lambda *n: pltpu.VMEM((*n, ROWS, LANES), BF)
    vm = lambda a, b, t: pltpu.VMEM((a, b), t)
    return pl.pallas_call(
        functools.partial(back_kernel, where),
        out_shape=(
            jax.ShapeDtypeStruct((window, D), BF), jax.ShapeDtypeStruct((rows, D), F32), jax.ShapeDtypeStruct(parts.shape, BF),
        ),
        in_specs=[ANY, VM, VM, ANY, VM, VM, VM, VM, VM, ANY],
        out_specs=[ANY, VM, ANY],
        scratch_shapes=[
            tiles(3, D // ROWS, DC), tiles(2), tiles(2), vm(window, rows, F32), vm(window, rows, F32), vm(window, rows, BF),
            vm(D, window, BF), vm(window, D, F32), vm(window, D, F32), vm(D, rows, F32), vm(PAIR, rows, F32), vm(LANES, rows, F32),
            vm(window, D, BF), dma((3,)), dma, dma, dma,
        ],
        input_output_aliases={9: 2},
        compiler_params=pltpu.CompilerParams(vmem_limit_bytes=VMEM_LIMIT),
        name="back",
    )(x_win, seg_query, seg_keys, gathered, queries, key_win, value_win, att_grad, logs, parts)


HOT_NAMES = ("vec1", "w_query", "w_key", "w_value", "vec2")


def transfer_pieces(plan, depth):
    where = plan[0]
    count = plan[2].shape[0]
    hot, used = [0] * depth, [0] * depth
    for name in where:
        for owner, at, tiles in where[name]:
            level = owner * depth // count
            used[level] = max(used[level], at + tiles)
            if name in HOT_NAMES:
                hot[level] = max(hot[level], at + tiles)
    early = [(level, 0, h) for level, h in enumerate(hot) if h]
    late = [(level, h, u - h) for level, (h, u) in enumerate(zip(hot, used)) if h < u]
    return early, late


def cut(piece, many):
    level, first, tiles = piece
    half = tiles // 2
    edges = [half * i // (many // 2) for i in range(many // 2)] + [
        half + (tiles - half) * i // (many // 2) for i in range(many // 2 + 1)
    ]
    return [(level, first + a, b - a) for a, b in zip(edges[:-1], edges[1:])]


def gather_front_kernel(
    depth, where, early, late,
    block_ref, x_in_ref, segq_ref, segk_ref,
    out_ref, x_out_ref, turned_out_ref, keys_out_ref, k_out_ref, v_out_ref, x_got_ref, q_ref, attended_ref, rest_ref, logs_ref,
    z_send, z_recv, x_send, x_recv, y_send, y_recv, corner_send, corner_recv, line_send, line_recv, mate_send, mate_recv, w_send, w_recv,
    local_sem, stage_ref, both_ref, x_ref, turned_ref, normed_ref, w_ref, vec1_ref, vec2_ref, bias_ref, score_ref, prob_ref, add_ref, sem, vec_sem, x_sem, keys_sem,
):
    me = lax.axis_index("fsdp")
    count = 8 * depth
    core, x, y, z = place(me)
    mate, x_near, y_near = index_of(1 - core, x, y, z), index_of(core, 1 - x, y, z), index_of(core, x, 1 - y, z)
    up, down = me + 8, me - 8
    after, before = me + 2, me - 2
    has_after, has_before = after < count, before >= 0
    greet(
        [(mate, None), (x_near, None), (y_near, None), (down, z > 0), (up, z < depth - 1), (after, has_after), (before, has_before)]
    )
    pieces = early + late
    chunks = {p: cut(piece, 4) if piece[0] == 0 and p < len(early) else [piece] for p, piece in enumerate(pieces)}
    chunk_list = [(p, chunk) for p in chunks for chunk in chunks[p]]
    ids = {p: [i for i, (q, _) in enumerate(chunk_list) if q == p] for p in chunks}
    hot, cold = range(len(early)), range(len(early), len(pieces))
    hot_levels = {level for level, _, _ in early}

    def remote(source, target, send, recv, device):
        return pltpu.make_async_remote_copy(
            src_ref=source, dst_ref=target, send_sem=send, recv_sem=recv, device_id=(device,), device_id_type=MESH
        )

    def span(piece):
        return pl.ds(piece[1], piece[2])

    def halves(p):
        level, first, tiles = pieces[p]
        part = tiles // 2 if p in hot else tiles * 2 // 3
        return (level, first, part), (level, first + part, tiles - part)

    def column(level):
        return index_of(core, x, y, level)

    def from_x(level):
        return index_of(core, 1 - x, y, level)

    def from_y(level):
        return index_of(core, x, 1 - y, level)

    def across(level):
        return index_of(core, 1 - x, 1 - y, level)

    def pass_on(block, piece, send, recv, device, own=False):
        there = out_ref.at[block, span(piece)]
        return remote(block_ref.at[span(piece)] if own else there, there, send, recv, device)

    def z_copy(i, upward, own=False):
        piece = chunk_list[i][1]
        return pass_on(column(piece[0]), piece, z_send.at[i, 0 if upward else 1], z_recv.at[i], up if upward else down, own)

    def plane_copies(i, own=False):
        piece = chunk_list[i][1]
        block = column(piece[0])
        return (
            pass_on(block, piece, x_send.at[i], x_recv.at[i], x_near, own),
            pass_on(block, piece, y_send.at[i], y_recv.at[i], y_near, own),
            pass_on(block, piece, mate_send.at[0, i], mate_recv.at[0, i], mate, own),
        )

    def got(block, i, recv):
        piece = chunk_list[i][1]
        pass_on(block, piece, x_send.at[i], recv, me).wait_recv()

    def spread(i, own=False):
        for copy in plane_copies(i, own):
            copy.start()

    def z_pass(i):
        def run(zv):
            level = chunk_list[i][1][0]
            got(column(level), i, z_recv.at[i])
            if level < zv < depth - 1:
                z_copy(i, True).start()
            if 0 < zv < level:
                z_copy(i, False).start()

        return run

    def take(i):
        def run(zv):
            z_pass(i)(zv)
            spread(i)

        return run

    def later_spread(i):
        return lambda zv: spread(i)

    def by_plane(p, zv):
        return True

    def corner_copies(p):
        level = pieces[p][0]
        first, second = halves(p)
        return (
            pass_on(from_x(level), first, corner_send.at[p, 0], corner_recv.at[p, 0], y_near),
            pass_on(from_y(level), second, corner_send.at[p, 1], corner_recv.at[p, 1], x_near),
        )

    def corner_along_z(p, zv):
        level = pieces[p][0]
        ways = [up] * (level <= zv < depth - 1) + [down] * (0 < zv <= level)
        return [
            [
                pass_on(across(level), part, line_send.at[p, 2 * side + (way is up)], line_recv.at[p, side], way)
                for way in ways
            ]
            for side, part in enumerate(halves(p))
        ]

    def mate_copies(p):
        level = pieces[p][0]
        first, second = halves(p)
        return (
            pass_on(from_x(level), pieces[p], mate_send.at[1, p], mate_recv.at[1, p], mate),
            pass_on(from_y(level), pieces[p], mate_send.at[2, p], mate_recv.at[2, p], mate),
            pass_on(across(level), first, mate_send.at[3, p], mate_recv.at[3, p], mate),
            pass_on(across(level), second, mate_send.at[4, p], mate_recv.at[4, p], mate),
        )

    def beside(p):
        def run(zv):
            level = pieces[p][0]
            for i in ids[p]:
                got(from_x(level), i, x_recv.at[i])
            if by_plane(p, zv):
                corner_copies(p)[0].start()
            mate_copies(p)[0].start()
            for i in ids[p]:
                got(from_y(level), i, y_recv.at[i])
            if by_plane(p, zv):
                corner_copies(p)[1].start()
            mate_copies(p)[1].start()

        return run

    def corner(p):
        def run(zv):
            level = pieces[p][0]
            for side, part in enumerate(halves(p)):
                recv = corner_recv if by_plane(p, zv) else line_recv
                pass_on(across(level), part, corner_send.at[p, side], recv.at[p, side], me).wait_recv()
                if not by_plane(p, zv):
                    for copy in corner_along_z(p, zv)[side]:
                        copy.start()
                mate_copies(p)[2 + side].start()

        return run

    def from_mate(p):
        def run(zv):
            level = pieces[p][0]
            other = 1 - 2 * core
            for i in ids[p]:
                pass_on(column(level) + other, chunk_list[i][1], mate_send.at[0, i], mate_recv.at[0, i], me).wait_recv()
            first, second = halves(p)
            for slot, (block, piece) in enumerate(
                ((from_x(level), pieces[p]), (from_y(level), pieces[p]), (across(level), first), (across(level), second))
            ):
                pass_on(block + other, piece, mate_send.at[slot + 1, p], mate_recv.at[slot + 1, p], me).wait_recv()

        return run

    def own_spread(i):
        return lambda zv: spread(i, True)

    def own_up(i):
        return lambda zv: z_copy(i, True, True).start() if zv < depth - 1 else None

    def own_down(i):
        return lambda zv: z_copy(i, False, True).start() if zv > 0 else None

    def w_copy(slot, which, device, source=None):
        return remote(x_in_ref if source is None else source, x_got_ref.at[slot], w_send.at[which], w_recv.at[slot], device)

    def w_far(zv):
        @pl.when(has_after)
        def _():
            w_copy(0, 1, after).start()

        @pl.when(has_before)
        def _():
            w_copy(4, 2, before).start()

    def w_forward(core_index):
        slot = 0 if core_index else 4
        return w_copy(1 if core_index else 3, 3, mate, x_got_ref.at[slot])

    def w_wait(slot):
        w_copy(slot, 0, me).wait_recv()

    def w_middle(zv):
        @pl.when(has_before)
        def _():
            w_wait(0)

        @pl.when(has_after)
        def _():
            w_wait(4)

        @pl.when((core == 1) & has_before)
        def _():
            w_forward(1).start()

        @pl.when((core == 0) & has_after)
        def _():
            w_forward(0).start()

    stops = [61.0, 63.0, 68.0, 73.0, 95.0, 102.0, 110.0] + [110.0 + 2.7 * h for h in range(1, HEADS)]

    def lists(zv):
        own_hot = [p for p in hot if pieces[p][0] == zv]
        own_cold = [p for p in cold if pieces[p][0] == zv]
        far_hot = sorted((p for p in hot if pieces[p][0] != zv), key=lambda p: abs(pieces[p][0] - zv))
        far_cold = sorted((p for p in cold if pieces[p][0] != zv), key=lambda p: (abs(pieces[p][0] - zv), -pieces[p][0]))
        distance = {p: abs(pieces[p][0] - zv) for p in cold}
        at_once = own_cold if zv > depth // 2 else []
        after_hot = [p for p in own_cold if p not in at_once]
        first = []
        for p in own_hot:
            for i in ids[p]:
                first += [own_up(i), own_down(i), own_spread(i)]
        for p in own_cold:
            first += [own_down(i) for i in ids[p]]
        for p in at_once:
            first += [own_spread(i) for i in ids[p]]
        for p in far_hot:
            first += [take(i) for i in ids[p]]
        passed = {p for p in far_cold if distance[p] < 3 and (0 < zv < pieces[p][0] or pieces[p][0] < zv < depth - 1)}
        from_above = [p for p in far_cold if p in passed and pieces[p][0] == zv + 1]
        first += [z_pass(i) for p in from_above for i in ids[p]]
        for p in own_cold:
            first += [own_up(i) for i in ids[p]]
        order_hot = own_hot + far_hot
        first += [beside(p) for p in order_hot]
        first += [z_pass(i) for p in far_cold if p in passed and p not in from_above for i in ids[p]]
        take_or_spread = lambda p: [(later_spread if p in passed else take)(i) for i in ids[p]]
        first.append(w_far)
        for p in after_hot:
            first += [own_spread(i) for i in ids[p]]
        for p in far_cold:
            first += take_or_spread(p) if distance[p] == 1 else []
        first += [corner(p) for p in order_hot]
        first += [from_mate(p) for p in order_hot]
        timed = [(73.0, event) for p in far_cold if distance[p] > 1 for event in take_or_spread(p)]
        order = at_once + after_hot + far_cold
        timed += [((110.0, 120.8, 137.0, 145.0)[min(k, 3)], beside(p)) for k, p in enumerate(order)]
        timed += [((142.4, 150.5, 200.0)[min(k, 2)], corner(p)) for k, p in enumerate(order)]
        return first, sorted(timed, key=lambda entry: entry[0])

    plans = [lists(zv) for zv in range(depth)]

    def each_plane(events_of):
        for zv in range(depth):
            events = events_of(zv)
            if events:

                @pl.when(z == zv)
                def _():
                    for event in events:
                        event(zv)

    w_copy(1 + 2 * core, 0, mate).start()
    fill = pltpu.make_async_copy(block_ref, stage_ref, local_sem)
    fill.start()
    fill.wait()
    keep = pltpu.make_async_copy(stage_ref, out_ref.at[me], local_sem)
    keep.start()
    each_plane(lambda zv: plans[zv][0])
    keep.wait()

    near_sem = x_sem
    def service(stop):
        low = stops[stop - 1] if stop else -1.0
        high = stops[stop] if stop < len(stops) else 1e9
        each_plane(lambda zv: [event for time, event in plans[zv][1] if low < time <= high])

    rows, window = q_ref.shape[0], x_ref.shape[0]
    k_ref, v_ref = both_ref.at[0], both_ref.at[1]
    loads = [copies(where, name, out_ref, w_ref.at[i], sem.at[i]) for i, name in enumerate(("w_query", "w_key", "w_value"))]
    vecs = copies(where, "vec1", out_ref, vec1_ref, vec_sem) + copies(where, "vec2", out_ref, vec2_ref, vec_sem)
    start(vecs)
    for made in loads:
        start(made)

    def slot_rows(slot):
        return pl.ds(pl.multiple_of(slot * rows, rows), rows)

    def bring(slot, there=None):
        at = x_ref.at[slot_rows(slot)]
        if there is None:
            pltpu.make_async_copy(x_got_ref.at[slot], at, near_sem).start()
            return

        @pl.when(there)
        def _():
            pltpu.make_async_copy(x_got_ref.at[slot], at, near_sem).start()

        @pl.when(jnp.logical_not(there))
        def _():
            pltpu.make_async_copy(x_in_ref, at, near_sem).start()

    def brought(many):
        for _ in range(many):
            pltpu.make_async_copy(x_in_ref, x_ref.at[slot_rows(0)], near_sem).wait()

    mate_slot, far_slot = 3 - 2 * core, 1 + 2 * core
    w_wait(mate_slot)
    pltpu.make_async_copy(x_in_ref, x_ref.at[slot_rows(2)], near_sem).start()
    bring(mate_slot)
    brought(2)
    wait(vecs)
    vec = vector_rows(vec1_ref)
    gain, shift = as_row(vec, 0, DC), as_row(vec, DC, DC)
    biases = vector_rows(vec2_ref)
    step = rows // 3

    @pl.loop(0, rows // 8)
    def _(i):
        at = pl.ds(i * 8, 8)
        bias_ref[at] = jnp.where(segq_ref[at] == segk_ref[...], 0.0, NEG)

    def over_slots(slots, body):
        @pl.loop(0, len(slots))
        def _(i):
            slot = slots[-1]
            for k, other in enumerate(slots[:-1]):
                slot = jnp.where(i == k, other, slot)
            body(slot)

    def norm_slots(slots):
        def norm_slot(slot):
            @pl.loop(0, rows // step)
            def _(i):
                at = pl.ds(pl.multiple_of(slot * rows + i * step, step), step)
                normed, _ = norm_rows(x_ref[at].astype(F32))
                turned_ref[:, at] = normed.astype(BF).T
                normed_ref[at] = (normed * gain + shift).astype(BF)

        over_slots(slots, norm_slot)

    def project(i, slots):
        def some(c, many):
            lanes = lanes_of(c, many)
            weights = panels(w_ref.at[i], c, many, D // ROWS)

            def rows_of(slot):
                value = (nn(normed_ref[slot_rows(slot)], weights) + add_ref[i, 0:1, lanes]).astype(BF)
                if isinstance(i, int):
                    q_ref[:, lanes] = value
                else:
                    both_ref[i - 1, slot_rows(slot), lanes] = value

            over_slots(slots, rows_of)

        over_pairs(some)

    def keys_and_values(slots, between):
        @pl.loop(0, 2)
        def _(i):
            project(i + 1, slots)
            for k, action in enumerate(between):

                @pl.when(i == k)
                def _():
                    action()

    norm_slots([2, mate_slot])
    service(0)
    for made in loads:
        wait(made)
    for i, row in enumerate((as_row(biases, 0, DC), jnp.zeros((1, D), F32), as_row(biases, DC, DC))):
        add_ref[i, 0:1] = row
    project(0, [2])
    service(1)
    keys_and_values([2, mate_slot], [lambda: service(2), lambda: service(3)])
    w_middle(None)

    @pl.when((core == 0) & has_before)
    def _():
        w_wait(1)

    @pl.when((core == 1) & has_after)
    def _():
        w_wait(3)

    bring(0, has_before)
    bring(4, has_after)
    bring(far_slot, jnp.where(core == 0, has_before, has_after))
    brought(3)
    others = [0, 4, far_slot]
    norm_slots(others)
    saves = [pltpu.make_async_copy(x_ref, x_out_ref, local_sem), pltpu.make_async_copy(turned_ref, turned_out_ref, local_sem)]
    start(saves)
    service(4)
    k_save = pltpu.make_async_copy(k_ref, k_out_ref, keys_sem.at[0])

    def keys_done():
        service(5)
        k_save.start()

    keys_and_values(others, [keys_done])
    v_save = pltpu.make_async_copy(v_ref, v_out_ref, keys_sem.at[1])
    v_save.start()
    wait(saves)

    @pl.loop(0, window // LANES)
    def _(i):
        at = pl.ds(pl.multiple_of(i * LANES, LANES), LANES)
        turned_ref[:, at] = k_ref[at].T

    keys_save = pltpu.make_async_copy(turned_ref, keys_out_ref, keys_sem.at[2])
    keys_save.start()
    attended_ref[...] = jnp.zeros_like(attended_ref)
    rest_ref[...] = jnp.zeros_like(rest_ref)
    logs_ref[...] = jnp.zeros_like(logs_ref)
    lane_l = lax.broadcasted_iota(jnp.int32, logs_ref.shape, 1)

    @pl.loop(0, HEADS)
    def _(h):
        for at_head in range(HEADS):

            @pl.when(h == at_head)
            def _():
                service(6 + at_head)

        lane, offset = head_window(h)
        mask = head_mask(rows, offset)
        lanes = pl.ds(lane, PAIR)
        query = jnp.where(mask, q_ref[:, lanes], jnp.zeros((), BF))
        score_ref[...] = nt(query, k_ref[:, lanes]) * SCALE + bias_ref[...]
        top = jnp.max(score_ref[...], axis=-1, keepdims=True)
        powers = jnp.exp(score_ref[...] - top)
        total = jnp.sum(powers, axis=-1, keepdims=True)
        prob_ref[...] = powers.astype(BF)
        out = nn(prob_ref[...], v_ref[:, lanes]) / total
        rounded = out.astype(BF)
        attended_ref[:, lanes] = jnp.where(mask, rounded, attended_ref[:, lanes])
        rest_ref[:, lanes] = jnp.where(mask, (out - rounded.astype(F32)).astype(BF), rest_ref[:, lanes])
        logs_ref[...] = jnp.where(lane_l == h, top + jnp.log(total), logs_ref[...])

    service(len(stops))
    each_plane(lambda zv: [from_mate(p) for p in cold])

    def sent(zv):
        for i, (p, piece) in enumerate(chunk_list):
            for copy in plane_copies(i):
                copy.wait_send()
            level = piece[0]
            if zv < depth - 1 and level <= zv:
                z_copy(i, True).wait_send()
            if zv > 0 and level >= zv:
                z_copy(i, False).wait_send()
        for p in range(len(pieces)):
            for copy in mate_copies(p) + (corner_copies(p) if by_plane(p, zv) else ()):
                copy.wait_send()
            for copy in sum(corner_along_z(p, zv), []) if not by_plane(p, zv) else []:
                copy.wait_send()

    each_plane(lambda zv: [sent])
    w_copy(0, 0, mate).wait_send()

    @pl.when(has_after)
    def _():
        w_copy(0, 1, after).wait_send()

    @pl.when(has_before)
    def _():
        w_copy(4, 2, before).wait_send()

    @pl.when(jnp.where(core == 1, has_before, has_after))
    def _():
        w_forward(0).wait_send()

    wait([k_save, v_save, keys_save])


def gather_front(block, block_input, seg_query, seg_keys, plan):
    where = plan[0]
    count = lax.axis_size("fsdp")
    depth = count // 8
    rows, window = block_input.shape[0], seg_keys.shape[1]
    early, whole = transfer_pieces(plan, depth)
    late = whole
    shape = lambda n, d=D, t=BF: jax.ShapeDtypeStruct((n, d), t)
    dma = pltpu.SemaphoreType.DMA
    units = D // ROWS
    many = len(early) + len(late)
    chunks = many + 3 * sum(1 for piece in early if piece[0] == 0)
    got = jax.ShapeDtypeStruct((5, rows, D), BF)
    return pl.pallas_call(
        functools.partial(gather_front_kernel, depth, where, early, late),
        out_shape=(
            jax.ShapeDtypeStruct((count, *block.shape), BF), shape(window), shape(D, window), shape(D, window), shape(window), shape(window), got,
            shape(rows), shape(rows), shape(rows), shape(rows, LANES, F32),
        ),
        in_specs=[ANY, ANY, VM, VM],
        out_specs=[ANY] * 7 + [VM] * 4,
        scratch_shapes=[
            dma((chunks, 2)), dma((chunks,)), dma((chunks,)), dma((chunks,)), dma((chunks,)), dma((chunks,)),
            dma((many, 2)), dma((many, 2)), dma((many, 4)), dma((many, 2)), dma((5, chunks)), dma((5, chunks)), dma((4,)), dma((5,)),
            dma, pltpu.VMEM(block.shape, BF), pltpu.VMEM((2, window, D), BF),
            pltpu.VMEM((window, D), BF), pltpu.VMEM((D, window), BF), pltpu.VMEM((window, D), BF),
            pltpu.VMEM((3, units, DC, ROWS, LANES), BF), pltpu.VMEM((2, ROWS, LANES), BF), pltpu.VMEM((2, ROWS, LANES), BF),
            pltpu.VMEM((rows, window), F32), pltpu.VMEM((rows, window), F32), pltpu.VMEM((rows, window), BF), pltpu.VMEM((3, 8, D), F32),
            dma((3,)), dma, dma, dma((3,)),
        ],
        compiler_params=pltpu.CompilerParams(collective_id=0, has_side_effects=True, vmem_limit_bytes=VMEM_LIMIT),
        name="gather_front",
    )(block, block_input, seg_query, seg_keys)


def back_scatter_kernel(
    depth, where, early, late,
    x_hbm_ref, turned_hbm_ref, keys_hbm_ref, segq_ref, segk_ref, blocks_ref, q_ref, k_hbm_ref, v_hbm_ref, grad_ref, logs_ref, delta_ref, mid_hbm_ref, parts_in_ref,
    parts_ref, out_ref, in_grad_ref, mates, sums, halfs, fulls, lines, near_ref, near_got,
    w_ref, g_ref, vec1_ref, vec2_ref, score_ref, prob_ref, turned_ref, k_ref, v_ref, dq_ref, part_ref, logs_t_ref, x_ref, dq_b_ref,
    block_ref, mid_ref, g_value_ref, gain_acc, shift_acc, stage, total,
    mate_send, mate_recv, half_send, half_recv, full_send, full_recv, line_send, line_recv, near_send, near_recv,
    load_sem, store_sem, sem, vec_sem, out_sem, x_sem,
):
    me = lax.axis_index("fsdp")
    count = 8 * depth
    core, x, y, z = place(me)
    mate, x_near, y_near = index_of(1 - core, x, y, z), index_of(core, 1 - x, y, z), index_of(core, x, 1 - y, z)
    after, before = me + 2, me - 2
    has_after, has_before = after < count, before >= 0
    greet(
        [(mate, None), (x_near, None), (y_near, None), (me - 8, z > 0), (me + 8, z < depth - 1), (after, has_after), (before, has_before)]
    )
    pieces = early + late
    block_tiles = parts_ref.shape[1]
    early_ids, late_ids = range(len(early)), range(len(early), len(pieces))

    def remote(source, target, send, recv, device):
        return pltpu.make_async_remote_copy(
            src_ref=source, dst_ref=target, send_sem=send, recv_sem=recv, device_id=(device,), device_id_type=MESH
        )

    def owner(level, slot, which_core):
        return index_of(which_core, 1 - x if slot in (1, 3) else x, 1 - y if slot in (2, 3) else y, level)

    def at_plane(zv, run):
        @pl.when(z == zv)
        def _():
            run()

    def span(p, lo=0, many=None):
        _, first, tiles = pieces[p]
        return pl.ds(first + lo, tiles if many is None else many)

    def half_of(p):
        return pieces[p][2] // 2

    def to_mate(p, slot):
        level = pieces[p][0]
        return remote(
            parts_ref.at[owner(level, slot, 1 - core), span(p)], mates.at[level, slot, span(p)],
            mate_send.at[p, slot], mate_recv.at[p, slot], mate,
        )

    def half_out(p, side):
        level, _, tiles = pieces[p]
        part = span(p, half_of(p), tiles - half_of(p)) if side else span(p, 0, half_of(p))
        return remote(
            sums.at[level, 3, part], halfs.at[level, side, part], half_send.at[p, side], half_recv.at[p, side],
            x_near if side else y_near,
        )

    def full_out(p, side):
        level = pieces[p][0]
        return remote(
            sums.at[level, 1 + side, span(p)], fulls.at[level, side, span(p)], full_send.at[p, side], full_recv.at[p, side],
            y_near if side else x_near,
        )

    def subs(p):
        tiles = pieces[p][2]
        if p in early_ids or tiles < block_tiles // 3:
            return [(0, tiles)]
        return [(0, tiles // 2), (tiles // 2, tiles - tiles // 2)]

    def line_out(p, zv, sub):
        level = pieces[p][0]
        part = span(p, *subs(p)[sub])
        upward = level > zv
        slot = depth if not upward and level == zv - 1 else level
        side = 1 if slot == depth else 0
        return remote(
            sums.at[level, 0, part], lines.at[slot, part], line_send.at[p, sub], line_recv.at[p, 2 * sub + side],
            me + 8 if upward else me - 8,
        )

    def line_in(p, side, sub):
        level = pieces[p][0]
        slot = depth if side else level
        part = span(p, *subs(p)[sub])
        return remote(sums.at[level, 0, part], lines.at[slot, part], line_send.at[p, sub], line_recv.at[p, 2 * sub + side], me)

    def line_sides(p, zv):
        level = pieces[p][0]
        if level > zv:
            return [0] if zv > 0 else []
        if level < zv:
            return [0] if zv < depth - 1 else []
        return ([0] if zv > 0 else []) + ([1] if zv < depth - 1 else [])

    def extent(job):
        kind, p, sub = job
        return subs(p)[sub] if kind == 0 else (0, pieces[p][2])

    def sources(job, zv):
        kind, p, sub = job
        level, _, tiles = pieces[p]
        h = half_of(p)
        if kind == 0:
            lo, many = extent(job)
            part = span(p, lo, many)
            refs = [parts_ref.at[owner(level, 0, core), part], mates.at[level, 0, part]]
            refs += [fulls.at[level, side, part] for side in (0, 1)]
            refs += [lines.at[depth if side else level, part] for side in line_sides(p, zv)]
            return [(ref, 0, many) for ref in refs]
        found = [(parts_ref.at[owner(level, kind, core), span(p)], 0, tiles), (mates.at[level, kind, span(p)], 0, tiles)]
        if kind == 1:
            found.append((halfs.at[level, 0, span(p, 0, h)], 0, h))
        if kind == 2:
            found.append((halfs.at[level, 1, span(p, h, tiles - h)], h, tiles - h))
        return found

    def loads(job, zv, base):
        return [
            pltpu.make_async_copy(ref, stage.at[i, pl.ds(base + lo, many)], load_sem.at[1 if base else 0])
            for i, (ref, lo, many) in enumerate(sources(job, zv))
        ]

    def store(job, base):
        kind, p, sub = job
        lo, many = extent(job)
        return pltpu.make_async_copy(
            total.at[pl.ds(base, many)], sums.at[pieces[p][0], kind, span(p, lo, many)], store_sem.at[1 if base else 0]
        )

    def load(job, zv, base=0):
        kind, p, sub = job
        if sub == 0:
            to_mate(p, kind).wait_recv()
        if kind in (1, 2):
            half_out(p, kind - 1).wait_recv()
        made = loads(job, zv, base)
        if kind == 0:
            if sub == 0:
                for side in (0, 1):
                    full_out(p, side).wait_recv()
            start(made[:4])
            for copy, side in zip(made[4:], line_sides(p, zv)):
                line_in(p, side, sub).wait_recv()
                copy.start()
        else:
            start(made)

    def add(base, lo, many, slots, target, shift):
        def some(first, tiles):
            value = stage[slots[0], pl.ds(first, tiles)].astype(F32)
            for slot in slots[1:]:
                value = value + stage[slot, pl.ds(first, tiles)].astype(F32)
            target[pl.ds(first + shift, tiles)] = value.astype(target.dtype)

        group = 8

        @pl.loop(0, many // group)
        def _(i):
            some(base + lo + i * group, group)

        if many % group:
            some(base + lo + many // group * group, many % group)

    def finish(job, zv, base=0):
        kind, p, sub = job
        level, first, tiles = pieces[p]
        found = sources(job, zv)
        wait(loads(job, zv, base))
        final = kind == 0 and level == zv
        target, shift = (out_ref, first + extent(job)[0] - base) if final else (total, 0)
        edges = sorted({e for _, lo, many in found for e in (lo, lo + many)})
        for lo, hi in zip(edges[:-1], edges[1:]):
            slots = [i for i, (_, a, many) in enumerate(found) if a <= lo and hi <= a + many]
            add(base, lo, hi - lo, slots, target, shift)
        if not final:
            store(job, base).start()

    def send(job, zv, base=0):
        kind, p, sub = job
        if kind == 0 and pieces[p][0] == zv:
            return
        store(job, base).wait()
        if kind == 3:
            half_out(p, 0).start()
            half_out(p, 1).start()
        elif kind == 0:
            line_out(p, zv, sub).start()
        else:
            full_out(p, kind - 1).start()

    second = block_tiles // 2

    def run(jobs, zv):
        for job in jobs:
            load(job, zv)
            finish(job, zv)
            send(job, zv)

    def run_ahead(jobs, zv):
        bases = [second * (k % 2) for k in range(len(jobs))]
        for k, job in enumerate(jobs):
            if k == 0:
                load(job, zv, bases[k])
            if k + 1 < len(jobs):
                load(jobs[k + 1], zv, bases[k + 1])
            finish(job, zv, bases[k])
            if k:
                send(jobs[k - 1], zv, bases[k - 1])
        send(jobs[-1], zv, bases[-1])

    def along(p):
        return [(0, p, sub) for sub in range(len(subs(p)))]

    for p in early_ids:
        for slot in (3, 1, 2, 0):
            to_mate(p, slot).start()

    window, rows = k_ref.shape[0], q_ref.shape[0]
    margin = (window - rows) // 2
    names = ("w_query", "w_key", "w_value")
    k_load = [
        pltpu.make_async_copy(a, b, vec_sem)
        for a, b in ((k_hbm_ref, k_ref), (v_hbm_ref, v_ref), (keys_hbm_ref, turned_ref))
    ]
    start(k_load)
    weight_loads = [copies(where, name, blocks_ref, w_ref.at[i], sem.at[i]) for i, name in enumerate(names)]
    vecs = copies(where, "vec1", blocks_ref, vec1_ref, sem.at[3])
    start(vecs)
    for made in weight_loads:
        start(made)
    x_load = [pltpu.make_async_copy(x_hbm_ref, x_ref, x_sem)]
    start(x_load)
    logs_t_ref[...] = logs_ref[...].T * LOG2E
    g_value_ref[...] = jnp.zeros_like(g_value_ref)

    by_level = {pieces[p][0]: p for p in early_ids}
    a, b, c_ = (by_level[level] for level in sorted(by_level, reverse=True)[:3])
    table = [
        (-1, 0, 3, a, None), (0, 1, 3, b, None), (3, 4, 1, a, None), (4, 5, 2, a, None), (5, 6, 3, c_, None),
        (6, 7, 1, b, None), (7, 8, 2, b, None), (11, 12, 0, a, 0), (12, 13, 1, c_, None), (13, 14, 2, c_, None),
    ]

    def beside(h, which, action):
        for entry in table:
            if entry[which] < 0:
                continue
            kind, p, zv = entry[2:]
            job = (kind, p, 0)
            there = h == entry[which]
            if zv is not None:
                there = there & (z == zv)

            @pl.when(there)
            def _():
                action(job, zv)

    wait(k_load)
    load((3, a, 0), None)

    @pl.loop(0, HEADS)
    def _(h):
        beside(h, 1, finish)
        lane, offset = head_window(h)
        mask = head_mask(rows, offset)
        lanes = pl.ds(lane, PAIR)
        query = jnp.where(mask, q_ref[:, lanes], jnp.zeros((), BF))
        grad = jnp.where(mask, grad_ref[:, lanes], jnp.zeros((), BF))
        log_row, delta_row = logs_t_ref[pl.ds(h, 1)], delta_ref[pl.ds(h, 1)]
        blocks = [pl.ds(n * rows, rows) for n in range(window // rows)]
        for keys in blocks:
            together = jnp.concatenate([segk_ref[keys]] * (rows // LANES), axis=1) == segq_ref[...]
            probs = jnp.exp2(jnp.where(together, nt(k_ref[keys, lanes], query) * (SCALE * LOG2E) - log_row, NEG))
            prob_ref[keys] = probs.astype(BF)
            score_ref[keys] = (probs * (nt(v_ref[keys, lanes], grad) - delta_row)).astype(BF)
        beside(h, 1, send)
        beside(h, 0, load)
        side = head_mask(rows, offset)

        @pl.loop(0, window // rows)
        def _(n):
            keys = pl.ds(pl.multiple_of(n * rows, rows), rows)
            dv = nn(prob_ref[keys], grad)
            g_value_ref[:, lanes] += column_sums(dv)
            v_ref[keys, lanes] = jnp.where(side, dv.astype(BF), v_ref[keys, lanes])
            dk = nn(score_ref[keys], query) * SCALE
            k_ref[keys, lanes] = jnp.where(side, dk.astype(BF), k_ref[keys, lanes])
        tile = (h * HEAD_DIM) // ROWS * ROWS
        part_ref[...] = nn(turned_ref[pl.ds(pl.multiple_of(tile, ROWS), part_ref.shape[0])], score_ref[...])
        at = pl.ds(pl.multiple_of(h * HEAD_DIM, 8), HEAD_DIM)
        dq_ref[at] = part_ref[pl.ds(pl.multiple_of(h * HEAD_DIM - tile, 8), HEAD_DIM)]

    turned_load = pltpu.make_async_copy(turned_hbm_ref, turned_ref, vec_sem)
    turned_load.start()
    dq = dq_ref[...].T * SCALE
    put_vectors(vec2_ref, [column_sums(dq), g_value_ref[...]])
    saves = copies(where, "vec2", parts_ref, vec2_ref, out_sem.at[3], out=True)
    dq_b_ref[...] = dq.astype(BF)
    wait(vecs)
    vec = vector_rows(vec1_ref)
    gain, shift = as_row(vec, 0, DC), as_row(vec, DC, DC)
    gain_t, shift_t = (jnp.broadcast_to(v, (8, D)).T[:, :1] for v in (gain, shift))
    wait(x_load)
    step = rows // 3

    turned_load.wait()
    for made in weight_loads:
        wait(made)
    gain_acc[...] = jnp.zeros_like(gain_acc)
    shift_acc[...] = jnp.zeros_like(shift_acc)

    def plane_job(what, entries):
        for zv, p in entries:

            def go():
                job = (0, p, 0)
                if what == "load":
                    load(job, zv)
                else:
                    finish(job, zv)
                    send(job, zv)

            at_plane(zv, go)

    own = turned_ref[:, pl.ds(margin, rows)]
    made = []
    first_jobs, last_jobs = [(1, a), (0, b), (3, b)], [(0, c_), (3, c_)]
    for i, (left, right_ref) in enumerate(((own, dq_b_ref), (turned_ref, k_ref), (turned_ref, v_ref))):
        if i == 1:
            plane_job("load", first_jobs)
        if i == 2:
            plane_job("end", first_jobs)
            plane_job("load", last_jobs)
            wait(made[0])

        def project_back(c, many):
            right = right_ref[:, lanes_of(c, many)]
            raw = nn(left[...], right)
            summed = column_sums(right.astype(F32))
            put_panels(g_ref.at[i % 2], c, gain_t * raw + shift_t * summed)
            weights = panels(w_ref.at[i], c, many, D // ROWS).astype(F32)
            scaled, shifted = weights * raw, weights * summed
            for j in range(many):
                part = slice(j * LANES, (j + 1) * LANES)
                gain_acc[...] += scaled[:, part]
                shift_acc[...] += shifted[:, part]

        over_pairs(project_back)
        made.append(copies(where, names[i], parts_ref, g_ref.at[i % 2], out_sem.at[i], out=True))
        start(made[i])
    put_vectors(vec1_ref, [column_sums(gain_acc[...].T), column_sums(shift_acc[...].T)])
    saves = saves + copies(where, "vec1", parts_ref, vec1_ref, out_sem.at[3], out=True)
    start(saves)
    plane_job("end", last_jobs)
    wait(saves + made[1] + made[2])
    for slots in ((3,), (1, 2), (0,)):
        for p in late_ids:
            for slot in slots:
                to_mate(p, slot).start()

    def slot_rows(n):
        return pl.ds(pl.multiple_of(n * rows, rows), rows)

    def row_block(n, own=False):
        first = n * rows

        def project_back(c, many):
            part = lambda i: panels(w_ref.at[i], 0, DC, many * LANES // ROWS, c * (LANES // ROWS))
            value = nt(k_ref[slot_rows(n)], part(1)) + nt(v_ref[slot_rows(n)], part(2))
            if own:
                value = value + nt(dq_b_ref[...], part(0))
            block_ref[:, lanes_of(c, many)] = value

        over_pairs(project_back)

        @pl.loop(0, rows // step)
        def _(i):
            here = pl.ds(pl.multiple_of(i * step, step), step)
            there = pl.ds(pl.multiple_of(first + i * step, step), step)
            normed, inverse = norm_rows(x_ref[there].astype(F32))
            result = norm_rows_back(block_ref[here], normed, inverse, gain)
            if own:
                block_ref[here] = result
            else:
                x_ref[there] = result.astype(BF)

    def near_rows(slot):
        return x_ref.at[pl.ds(slot * rows, rows)]

    def near_save(slot):
        return pltpu.make_async_copy(near_rows(slot), near_ref.at[slot], x_sem)

    def near_copy(slot, which, device):
        return remote(near_ref.at[slot], near_got.at[which], near_send.at[which], near_recv.at[which], device)


    @pl.loop(0, 4)
    def _(i):
        row_block(jnp.where(i == 0, 0, jnp.where(i == 1, 4, 2 * i - 3)))

        @pl.when(i == 0)
        def _():
            run_ahead([(3, p, 0) for p in late_ids], None)

        @pl.when(i == 1)
        def _():
            at_plane(1, lambda: run([(0, b, 0)], 1))
            at_plane(2, lambda: run([(0, a, 0), (0, c_, 0)], 2))
            for p in late_ids:
                run_ahead([(1, p, 0), (2, p, 0)], None)

    sides = [near_save(slot) for slot in (0, 4, 1, 3)]
    start(sides)
    wait(sides)
    to_mate_itself, to_mate_shared = (3 - 2 * core), (1 + 2 * core)
    near_copy(to_mate_itself, 0, mate).start()
    near_copy(to_mate_shared, 1, mate).start()

    @pl.when((core == 0) & has_before)
    def _():
        near_copy(0, 2, before).start()

    @pl.when((core == 1) & has_after)
    def _():
        near_copy(4, 3, after).start()

    row_block(2, True)
    near_copy(0, 1, me).wait_recv()
    shared_slot = 4 - 4 * core
    fetch = pltpu.make_async_copy(near_got.at[1], k_ref.at[pl.ds(0, rows)], x_sem)
    fetch.start()
    fetch.wait()

    @pl.loop(0, rows // step)
    def _(i):
        here = pl.ds(pl.multiple_of(i * step, step), step)
        there = pl.ds(pl.multiple_of(shared_slot * rows + i * step, step), step)
        x_ref[there] = (x_ref[there].astype(F32) + k_ref[here].astype(F32)).astype(BF)

    shared_save = near_save(shared_slot)
    shared_save.start()
    shared_save.wait()

    @pl.when((core == 0) & has_after)
    def _():
        near_copy(4, 3, after).start()

    @pl.when((core == 1) & has_before)
    def _():
        near_copy(0, 2, before).start()

    def tail(zv):
        out = [p for p in late_ids if pieces[p][0] != zv]
        hops = lambda p: zv if pieces[p][0] > zv else depth - 1 - zv
        moving = [job for p in sorted(out, key=lambda p: (hops(p), p)) for job in along(p)]
        own = [p for ids in (early_ids, late_ids) for p in ids if pieces[p][0] == zv]
        return moving + [job for p in own for job in along(p)]

    for zv in range(depth):
        at_plane(zv, lambda: run(tail(zv), zv))

    near_copy(0, 0, me).wait_recv()

    @pl.when(has_after)
    def _():
        near_copy(0, 2, me).wait_recv()

    @pl.when(has_before)
    def _():
        near_copy(0, 3, me).wait_recv()

    for i, (which, there) in enumerate(((0, None), (2, has_after), (3, has_before))):
        target = k_ref.at[pl.ds(i * rows, rows)]
        if there is None:
            pltpu.make_async_copy(near_got.at[which], target, x_sem).start()
            continue

        @pl.when(there)
        def _():
            pltpu.make_async_copy(near_got.at[which], target, x_sem).start()

        @pl.when(jnp.logical_not(there))
        def _():
            pltpu.make_async_copy(near_ref.at[0], target, x_sem).start()

    for i in range(3):
        pltpu.make_async_copy(near_got.at[0], k_ref.at[pl.ds(i * rows, rows)], x_sem).wait()
    near_after, near_before = (jnp.where(there, 1.0, 0.0) for there in (has_after, has_before))

    @pl.loop(0, rows // step)
    def _(i):
        here = pl.ds(pl.multiple_of(i * step, step), step)
        fetch_mid = pltpu.make_async_copy(mid_hbm_ref.at[here], mid_ref, x_sem)
        fetch_mid.start()
        fetch_mid.wait()
        value = mid_ref[...] + block_ref[here] + k_ref[here].astype(F32)
        value = value + near_after * k_ref[pl.ds(pl.multiple_of(rows + i * step, step), step)].astype(F32)
        value = value + near_before * k_ref[pl.ds(pl.multiple_of(2 * rows + i * step, step), step)].astype(F32)
        in_grad_ref[here] = value.astype(BF)

    for p in range(len(pieces)):
        for slot in range(4):
            to_mate(p, slot).wait_send()
        for side in (0, 1):
            half_out(p, side).wait_send()
            full_out(p, side).wait_send()
        for zv in range(depth):
            if pieces[p][0] != zv:
                at_plane(zv, lambda: [line_out(p, zv, sub).wait_send() for sub in range(len(subs(p)))])
    near_copy(0, 0, mate).wait_send()
    near_copy(0, 1, mate).wait_send()

    @pl.when(has_before)
    def _():
        near_copy(0, 2, before).wait_send()

    @pl.when(has_after)
    def _():
        near_copy(4, 3, after).wait_send()


def back_scatter(x_win, turned, turned_keys, seg_query, seg_keys, gathered, queries, key_win, value_win, att_grad, logs, delta, mid_grad, parts, plan):
    where, block = plan[:2]
    window, rows = x_win.shape[0], queries.shape[0]
    seg_keys = jnp.broadcast_to(seg_keys, (window, LANES))
    count = lax.axis_size("fsdp")
    depth = count // 8
    hot, cold = transfer_pieces(plan, depth)
    early = sorted(cold, reverse=True)
    late = []
    for piece in sorted(hot, reverse=True):
        late += cut(piece, 2) if piece[2] > block // 2 else [piece]
    many = len(early) + len(late)
    dma = pltpu.SemaphoreType.DMA
    tiles = lambda *n: pltpu.VMEM((*n, ROWS, LANES), BF)
    vm = lambda a, b, t: pltpu.VMEM((a, b), t)
    hbm = lambda *n: jax.ShapeDtypeStruct((*n, ROWS, LANES), BF)
    return pl.pallas_call(
        functools.partial(back_scatter_kernel, depth, where, early, late),
        out_shape=(
            jax.ShapeDtypeStruct(parts.shape, BF), jax.ShapeDtypeStruct((block, ROWS, LANES), F32), jax.ShapeDtypeStruct((rows, D), BF),
            hbm(depth, 4, block), hbm(depth, 4, block), hbm(depth, 2, block), hbm(depth, 2, block), hbm(depth + 1, block),
            jax.ShapeDtypeStruct((5, rows, D), BF), jax.ShapeDtypeStruct((4, rows, D), BF),
        ),
        in_specs=[ANY, ANY, ANY, VM, VM, ANY, VM, ANY, ANY, VM, VM, VM, ANY, ANY],
        out_specs=[ANY, VM, VM] + [ANY] * 7,
        scratch_shapes=[
            tiles(3, D // ROWS, DC), tiles(2, D // ROWS, DC), tiles(2), tiles(2),
            vm(window, rows, BF), vm(window, rows, BF), vm(D, window, BF), vm(window, D, BF), vm(window, D, BF),
            vm(D, rows, F32), vm(ROWS * pl.cdiv(HEAD_DIM + 8, ROWS), rows, F32), vm(LANES, rows, F32), vm(window, D, BF), vm(rows, D, BF), vm(rows, D, F32), vm(rows // 3, D, F32),
            vm(1, D, F32), vm(D, LANES, F32), vm(D, LANES, F32), tiles(6, block), tiles(block),
            dma((many, 4)), dma((many, 4)), dma((many, 2)), dma((many, 2)), dma((many, 2)), dma((many, 2)), dma((many, 2)), dma((many, 4)),
            dma((4,)), dma((4,)), dma((2,)), dma((2,)), dma((4,)), dma, dma((4,)), dma,
        ],
        input_output_aliases={13: 0},
        compiler_params=pltpu.CompilerParams(collective_id=1, has_side_effects=True, vmem_limit_bytes=VMEM_LIMIT),
        name="back_scatter",
    )(x_win, turned, turned_keys, seg_query, seg_keys, gathered, queries, key_win, value_win, att_grad, logs, delta, mid_grad, parts)[1:3]


def passed_along(value, steps):
    count = lax.axis_size("fsdp")
    first, last = (max(0, -steps), min(count, count - steps))
    return lax.ppermute(value, "fsdp", [(source, source + steps) for source in range(first, last)])


def window_of(rows):
    near = [rows if k == 0 else passed_along(rows, -k) for k in range(-REACH, REACH + 1)]
    return jnp.concatenate(near, axis=0)


def shards(kernels, block_input, params, cotangent, segment_ids):
    count = lax.axis_size("fsdp")
    me = lax.axis_index("fsdp")
    rows = block_input.shape[0]
    margin = REACH * rows
    seg_pad = jnp.pad(segment_ids, (margin, margin), constant_values=-1)
    seg_query = lax.dynamic_slice_in_dim(segment_ids, me * rows, rows, 0)
    seg_keys = lax.dynamic_slice_in_dim(seg_pad, me * rows, 2 * margin + rows, 0)
    plan = wire_plan(count, params.shape[1])
    where = plan[0]
    block = to_tiles(params, plan)
    if kernels:
        gathered, x_win, turned, turned_keys, key_win, value_win, _, queries, attended, rest, logs = gather_front(
            block, block_input, seg_query[:, None], seg_keys[None, :], plan
        )
    else:
        x_win = window_of(block_input)
        gathered = lax.all_gather(block, "fsdp", axis=0, tiled=False)
        queries, key_win, value_win, attended, rest, logs = front(
            x_win, seg_query[:, None], seg_keys[None, :], gathered, where, rows
        )
    activations, mid_grad, att_grad, delta, parts = middle(block_input, cotangent, attended, rest, gathered, where)
    sides = (seg_query[None, :], seg_keys[:, None], gathered, queries, key_win, value_win, att_grad, logs)
    if kernels:
        summed, input_grad = back_scatter(x_win, turned, turned_keys, *sides, delta, mid_grad, parts, plan)
    else:
        near, own, parts = back(x_win, *sides, parts, where)
        input_grad = mid_grad + own
        for k in range(-REACH, REACH + 1):
            if k != 0:
                part = near[(k + REACH) * rows : (k + REACH + 1) * rows]
                input_grad = input_grad + passed_along(part, k).astype(jnp.float32)
        input_grad = input_grad.astype(jnp.bfloat16)
        received = lax.all_to_all(parts, "fsdp", split_axis=0, concat_axis=0, tiled=True)
        summed = jnp.sum(received.astype(jnp.float32), axis=0)
    param_grads = to_flat(summed, plan, params.shape[1])
    return (activations, input_grad, param_grads)


def two_by_two(mesh):
    spans = np.array([device.coords for device in mesh.devices.flat])
    return tuple(spans.max(axis=0) - spans.min(axis=0))[:2] == (1, 1)


def solution(mesh):
    return jax.shard_map(
        functools.partial(shards, two_by_two(mesh)),
        mesh=mesh,
        in_specs=(P("fsdp", None), P(None, "fsdp"), P("fsdp", None), P()),
        out_specs=(P("fsdp", None), P("fsdp", None), P(None, "fsdp")),
        check_vma=False,
    )
```

profile of v0, /device:TPU:0, one launch (start us, length us, event | category | flops | bytes accessed | tf_op | source)
XLA Modules:
  0.0 501.9 jit_solution(9601324433941090057)
XLA Ops:
  0.6 1.2 slice.3
  1.9 6.5 %collective-permute-start = (bf16[1,69632]{1,0:T(2,128)(2,1)S(1)}, bf16[1,69632]{1,0:T(2,128)(2,1)S(1)}, u32[]{:S(2)}, u32[]{:S(2)}) collective-permute-start(bf16[1,69632]{1,0:T(2,128)(2,1)S(1)} %slice.3), channel_id=1, source_target_pairs={{0,31},{1,0},{2,1},{3,2},{4,3},{5,4},{6,5},{7,6},{8,7},{9,8},{10,9... | collective-permute-start | bytes 417800 | tf_op jit(solution)/shard_map/ppermute | solution.py:246
  8.3 0.8 pad_dynamic-slice_fusion
  9.1 1.3 fusion.table_ref
  10.4 0.8 dynamic_slice.19
  11.2 0.8 broadcast_in_dim.19.segq_ref
  12.0 0.6 broadcast_in_dim.17.segq_ref
  12.5 0.6 broadcast_in_dim.16.segk_ref
  13.1 1.3 fusion.2.table_ref
  14.4 0.0 collective-permute-done.head_ref
  14.4 0.0 copy-start.1
  14.4 0.7 copy-done.1
  15.1 7.8 %to_tiles.1.block_ref = bf16[242,16,128]{2,1,0:T(8,128)(2,1)} custom-call(s32[81]{0:T(128)} %fusion.table_ref, bf16[1,476288]{1,0:T(2,128)(2,1)} %line_ref.1, bf16[1,69632]{1,0:T(2,128)(2,1)} %copy-done.1), custom_call_target="tpu_custom_call" | custom-call | tf_op jit(solution)/shard_map/to_tiles/pallas_call | solution.py:248
  22.9 172.7 %gather_front.1 = (bf16[32,242,16,128]{3,2,1,0:T(8,128)(2,1)}, bf16[1920,1152]{1,0:T(8,128)(2,1)}, bf16[1152,1920]{1,0:T(8,128)(2,1)}, bf16[1152,1920]{1,0:T(8,1...) custom-call(bf16[242,16,128]{2,1,0:T(8,128)(2,1)} %to_tiles.1.block_, ...), custom_call_target="tpu_custom_call" | custom-call | tf_op jit(solution)/shard_map/gather_front/pallas_call | solution.py:1319
  195.6 56.6 %middle.1 = (bf16[384,1152]{1,0:T(8,128)(2,1)}, f32[384,1152]{1,0:T(8,128)}, bf16[384,1152]{1,0:T(8,128)(2,1)}, f32[16,384]{1,0:T(8,128)}, bf16[32,242,16,128]{3,2,1,0:T(8,128)(2,1)}) custom-call(bf16[384,1152]{1,0:T(8,128)(2,1)} %x_ref.1, bf16[384,1152]{1,0:T(8,128)(2,1)} %cot_ref.1, bf16[384,1152]{1,0:T(8,128)(2,1)} %get-tuple-element.20.attended_ref, ...), custom_call_target="tpu_custom_call" | custom-call | tf_op jit(solution)/shard_map/middle/pallas_call | solution.py:640
  252.2 1.3 broadcast_in_dim.18.segk_ref
  253.5 225.2 %back_scatter.1 = (bf16[32,242,16,128]{3,2,1,0:T(8,128)(2,1)}, f32[242,16,128]{2,1,0:T(8,128)}, bf16[384,1152]{1,0:T(8,128)(2,1)}, bf16[4,4,242,16,128]{4,3,2,1,...) custom-call(bf16[1920,1152]{1,0:T(8,128)(2,1)} %get-tuple-element.24, ...), custom_call_target="tpu_custom_call", output_to_operand_aliasing={{0}: (13, {})} | custom-call | tf_op jit(solution)/shard_map/back_scatter/pallas_call | solution.py:1878
  478.6 0.0 copy-start
  478.7 3.5 tail.1
  482.2 0.5 collective-permute-start.1
  482.7 1.2 fusion.1.table_ref
  483.9 8.1 %collective-permute-done.1.refs_0_ = f32[1,69632]{1,0:T(1,128)S(1)} collective-permute-done((f32[1,69632]{1,0:T(1,128)}, f32[1,69632]{1,0:T(1,128)S(1)}, u32[]{:S(2)}, u32[]{:S(2)}) %collective-permute-start.1) | collective-permute-done | bytes 278560 | tf_op jit(solution)/shard_map/ppermute | solution.py:280
  491.9 0.0 copy-start.2
  491.9 0.7 copy-done.2
  492.6 8.3 %to_flat.1 = f32[1,476288]{1,0:T(1,128)} custom-call(s32[82]{0:T(128)} %fusion.1.table_ref, f32[242,16,128]{2,1,0:T(8,128)} %get-tuple-element.36.tile_ref, f32[1,69632]{1,0:T(1,128)} %copy-done.2), custom_call_target="tpu_custom_call" | custom-call | tf_op jit(solution)/shard_map/to_flat/pallas_call | solution.py:269
  501.0 0.0 copy-done
  501.0 0.9 copy.14
Async XLA Ops:
  1.9 12.5 %collective-permute-start = (bf16[1,69632]{1,0:T(2,128)(2,1)S(1)}, bf16[1,69632]{1,0:T(2,128)(2,1)S(1)}, u32[]{:S(2)}, u32[]{:S(2)}) collective-permute-start(bf16[1,69632]{1,0:T(2,128)(2,1)S(1)} %slice.3), channel_id=1, source_target_pairs={{0,31},{1,0},{2,1},{3,2},{4,3},{5,4},{6,5},{7,6},{8,7},{9,8},{10,9... | collective-permute-start | bytes 417800 | tf_op jit(solution)/shard_map/ppermute | solution.py:246
  14.4 0.7 copy-start.1
  478.6 22.3 %copy-start = (bf16[384,1152]{1,0:T(8,128)(2,1)S(1)}, bf16[384,1152]{1,0:T(8,128)(2,1)}, u32[]{:S(2)}) copy-start(bf16[384,1152]{1,0:T(8,128)(2,1)} %get-tuple-element.41) | copy-start | bytes 2654212
  482.2 9.8 %collective-permute-start.1 = (f32[1,69632]{1,0:T(1,128)}, f32[1,69632]{1,0:T(1,128)S(1)}, u32[]{:S(2)}, u32[]{:S(2)}) collective-permute-start(f32[1,69632]{1,0:T(1,128)} %tail.1), channel_id=1, source_target_pairs={{0,1},{1,2},{2,3},{3,4},{4,5},{5,6},{6,7},{7,8},{8,9},{9,10},{10,1... | collective-permute-start | bytes 835592 | tf_op jit(solution)/shard_map/ppermute | solution.py:280
  491.9 0.7 copy-start.2
where the time goes:
time: 503 us; the launch traced here: 502 us
  Pallas kernels  474 us (94%)
  local copies, waits for them, and re-layouts  12.1 us (2%)
  waiting for transfers between devices  8.07 us (2%)
  starting transfers between devices  7 us (1%)
    pallas_call x1, Pallas kernels, back_scatter(): pl.pallas_call(functools.partial(back_scatter_kernel, depth, where, early...  225 us
    pallas_call x1, Pallas kernels, gather_front(): pl.pallas_call(functools.partial(gather_front_kernel, depth, where, early...  173 us
    pallas_call x1, Pallas kernels, middle(): pl.pallas_call(functools.partial(middle_kernel, where), out_shape=(shape(...  56.6 us
    pallas_call x2, Pallas kernels, call(): pl.pallas_call(functools.partial(to_flat_kernel, entries, rows), out_shap...  11.8 us
  transfers between devices with their start and end apart: 2, of which 1 were waited for; matrix products, arithmetic and copies ran while one was open for 1% of the time, Pallas kernels for 0%

commit v1 on v0

--- a/solution.py
+++ b/solution.py
@@ -1764,7 +1764,6 @@
     def _():
         near_copy(4, 3, after).start()
 
-    row_block(2, True)
     near_copy(0, 1, me).wait_recv()
     shared_slot = 4 - 4 * core
     fetch = pltpu.make_async_copy(near_got.at[1], k_ref.at[pl.ds(0, rows)], x_sem)
@@ -1789,43 +1788,19 @@
     def _():
         near_copy(0, 2, before).start()
 
-    def tail(zv):
-        out = [p for p in late_ids if pieces[p][0] != zv]
-        hops = lambda p: zv if pieces[p][0] > zv else depth - 1 - zv
-        moving = [job for p in sorted(out, key=lambda p: (hops(p), p)) for job in along(p)]
+    def hops(p, zv):
+        return zv if pieces[p][0] > zv else depth - 1 - zv
+
+    def tail(zv, at_end):
+        out = sorted((p for p in late_ids if pieces[p][0] != zv), key=lambda p: (hops(p, zv), p))
+        if not at_end:
+            return [job for p in out if hops(p, zv) == 0 for job in along(p)]
         own = [p for ids in (early_ids, late_ids) for p in ids if pieces[p][0] == zv]
-        return moving + [job for p in own for job in along(p)]
-
-    for zv in range(depth):
-        at_plane(zv, lambda: run(tail(zv), zv))
-
-    near_copy(0, 0, me).wait_recv()
-
-    @pl.when(has_after)
-    def _():
-        near_copy(0, 2, me).wait_recv()
-
-    @pl.when(has_before)
-    def _():
-        near_copy(0, 3, me).wait_recv()
-
-    for i, (which, there) in enumerate(((0, None), (2, has_after), (3, has_before))):
-        target = k_ref.at[pl.ds(i * rows, rows)]
-        if there is None:
-            pltpu.make_async_copy(near_got.at[which], target, x_sem).start()
-            continue
-
-        @pl.when(there)
-        def _():
-            pltpu.make_async_copy(near_got.at[which], target, x_sem).start()
-
-        @pl.when(jnp.logical_not(there))
-        def _():
-            pltpu.make_async_copy(near_ref.at[0], target, x_sem).start()
-
-    for i in range(3):
-        pltpu.make_async_copy(near_got.at[0], k_ref.at[pl.ds(i * rows, rows)], x_sem).wait()
-    near_after, near_before = (jnp.where(there, 1.0, 0.0) for there in (has_after, has_before))
+        return [job for p in out + own if p in own or hops(p, zv) for job in along(p)]
+
+    for zv in (0, depth - 1):
+        at_plane(zv, lambda: run(tail(zv, False), zv))
+    row_block(2, True)
 
     @pl.loop(0, rows // step)
     def _(i):
@@ -1833,7 +1808,43 @@
         fetch_mid = pltpu.make_async_copy(mid_hbm_ref.at[here], mid_ref, x_sem)
         fetch_mid.start()
         fetch_mid.wait()
-        value = mid_ref[...] + block_ref[here] + k_ref[here].astype(F32)
+        block_ref[here] += mid_ref[...]
+
+    for zv in range(depth):
+        at_plane(zv, lambda: run(tail(zv, True), zv))
+
+    near_copy(0, 0, me).wait_recv()
+
+    @pl.when(has_after)
+    def _():
+        near_copy(0, 2, me).wait_recv()
+
+    @pl.when(has_before)
+    def _():
+        near_copy(0, 3, me).wait_recv()
+
+    for i, (which, there) in enumerate(((0, None), (2, has_after), (3, has_before))):
+        target = k_ref.at[pl.ds(i * rows, rows)]
+        if there is None:
+            pltpu.make_async_copy(near_got.at[which], target, x_sem).start()
+            continue
+
+        @pl.when(there)
+        def _():
+            pltpu.make_async_copy(near_got.at[which], target, x_sem).start()
+
+        @pl.when(jnp.logical_not(there))
+        def _():
+            pltpu.make_async_copy(near_ref.at[0], target, x_sem).start()
+
+    for i in range(3):
+        pltpu.make_async_copy(near_got.at[0], k_ref.at[pl.ds(i * rows, rows)], x_sem).wait()
+    near_after, near_before = (jnp.where(there, 1.0, 0.0) for there in (has_after, has_before))
+
+    @pl.loop(0, rows // step)
+    def _(i):
+        here = pl.ds(pl.multiple_of(i * step, step), step)
+        value = block_ref[here] + k_ref[here].astype(F32)
         value = value + near_after * k_ref[pl.ds(pl.multiple_of(rows + i * step, step), step)].astype(F32)
         value = value + near_before * k_ref[pl.ds(pl.multiple_of(2 * rows + i * step, step), step)].astype(F32)
         in_grad_ref[here] = value.astype(BF)

time: 503 us -> 500 us (level)
  no operation moved by 1% of the time
where the time goes in v1:
time: 500 us; the launch traced here: 498 us
  Pallas kernels  471 us (94%)
  local copies, waits for them, and re-layouts  12.1 us (2%)
  waiting for transfers between devices  7.67 us (2%)
  starting transfers between devices  7.4 us (1%)
    pallas_call x1, Pallas kernels, back_scatter(): pl.pallas_call(functools.partial(back_scatter_kernel, depth, where, early...  222 us
    pallas_call x1, Pallas kernels, gather_front(): pl.pallas_call(functools.partial(gather_front_kernel, depth, where, early...  173 us
    pallas_call x1, Pallas kernels, middle(): pl.pallas_call(functools.partial(middle_kernel, where), out_shape=(shape(...  56.6 us
    pallas_call x2, Pallas kernels, call(): pl.pallas_call(functools.partial(to_flat_kernel, entries, rows), out_shap...  11.8 us
  transfers between devices with their start and end apart: 2, of which 1 were waited for; matrix products, arithmetic and copies ran while one was open for 1% of the time, Pallas kernels for 0%

profile of v1, /device:TPU:0, one launch (start us, length us, event | category | flops | bytes accessed | tf_op | source)
XLA Modules:
  0.0 498.3 jit_solution(3513982877464384759)
XLA Ops:
  0.6 1.2 slice.3
  1.9 6.5 %collective-permute-start = (bf16[1,69632]{1,0:T(2,128)(2,1)S(1)}, bf16[1,69632]{1,0:T(2,128)(2,1)S(1)}, u32[]{:S(2)}, u32[]{:S(2)}) collective-permute-start(bf16[1,69632]{1,0:T(2,128)(2,1)S(1)} %slice.3), channel_id=1, source_target_pairs={{0,31},{1,0},{2,1},{3,2},{4,3},{5,4},{6,5},{7,6},{8,7},{9,8},{10,9... | collective-permute-start | bytes 417800 | tf_op jit(solution)/shard_map/ppermute | solution.py:246
  8.3 0.8 pad_dynamic-slice_fusion
  9.1 1.3 fusion.table_ref
  10.4 0.8 dynamic_slice.19
  11.2 0.8 broadcast_in_dim.19.segq_ref
  12.0 0.6 broadcast_in_dim.17.segq_ref
  12.5 0.6 broadcast_in_dim.16.segk_ref
  13.1 1.3 fusion.2.table_ref
  14.4 0.0 collective-permute-done.head_ref
  14.4 0.0 copy-start.1
  14.4 0.7 copy-done.1
  15.1 7.8 %to_tiles.1.block_ref = bf16[242,16,128]{2,1,0:T(8,128)(2,1)} custom-call(s32[81]{0:T(128)} %fusion.table_ref, bf16[1,476288]{1,0:T(2,128)(2,1)} %line_ref.1, bf16[1,69632]{1,0:T(2,128)(2,1)} %copy-done.1), custom_call_target="tpu_custom_call" | custom-call | tf_op jit(solution)/shard_map/to_tiles/pallas_call | solution.py:248
  22.9 172.7 %gather_front.1 = (bf16[32,242,16,128]{3,2,1,0:T(8,128)(2,1)}, bf16[1920,1152]{1,0:T(8,128)(2,1)}, bf16[1152,1920]{1,0:T(8,128)(2,1)}, bf16[1152,1920]{1,0:T(8,1...) custom-call(bf16[242,16,128]{2,1,0:T(8,128)(2,1)} %to_tiles.1.block_, ...), custom_call_target="tpu_custom_call" | custom-call | tf_op jit(solution)/shard_map/gather_front/pallas_call | solution.py:1319
  195.6 56.6 %middle.1 = (bf16[384,1152]{1,0:T(8,128)(2,1)}, f32[384,1152]{1,0:T(8,128)}, bf16[384,1152]{1,0:T(8,128)(2,1)}, f32[16,384]{1,0:T(8,128)}, bf16[32,242,16,128]{3,2,1,0:T(8,128)(2,1)}) custom-call(bf16[384,1152]{1,0:T(8,128)(2,1)} %x_ref.1, bf16[384,1152]{1,0:T(8,128)(2,1)} %cot_ref.1, bf16[384,1152]{1,0:T(8,128)(2,1)} %get-tuple-element.20.attended_ref, ...), custom_call_target="tpu_custom_call" | custom-call | tf_op jit(solution)/shard_map/middle/pallas_call | solution.py:640
  252.2 1.3 broadcast_in_dim.18.segk_ref
  253.5 221.6 %back_scatter.1 = (bf16[32,242,16,128]{3,2,1,0:T(8,128)(2,1)}, f32[242,16,128]{2,1,0:T(8,128)}, bf16[384,1152]{1,0:T(8,128)(2,1)}, bf16[4,4,242,16,128]{4,3,2,1,...) custom-call(bf16[1920,1152]{1,0:T(8,128)(2,1)} %get-tuple-element.24, ...), custom_call_target="tpu_custom_call", output_to_operand_aliasing={{0}: (13, {})} | custom-call | tf_op jit(solution)/shard_map/back_scatter/pallas_call | solution.py:1889
  475.1 0.0 copy-start
  475.1 3.5 tail.1
  478.6 0.9 collective-permute-start.1
  479.5 1.2 fusion.1.table_ref
  480.7 7.7 %collective-permute-done.1.refs_0_ = f32[1,69632]{1,0:T(1,128)S(1)} collective-permute-done((f32[1,69632]{1,0:T(1,128)}, f32[1,69632]{1,0:T(1,128)S(1)}, u32[]{:S(2)}, u32[]{:S(2)}) %collective-permute-start.1) | collective-permute-done | bytes 278560 | tf_op jit(solution)/shard_map/ppermute | solution.py:280
  488.4 0.0 copy-start.2
  488.4 0.7 copy-done.2
  489.1 8.3 %to_flat.1 = f32[1,476288]{1,0:T(1,128)} custom-call(s32[82]{0:T(128)} %fusion.1.table_ref, f32[242,16,128]{2,1,0:T(8,128)} %get-tuple-element.36.tile_ref, f32[1,69632]{1,0:T(1,128)} %copy-done.2), custom_call_target="tpu_custom_call" | custom-call | tf_op jit(solution)/shard_map/to_flat/pallas_call | solution.py:269
  497.4 0.0 copy-done
  497.4 0.9 copy.14
Async XLA Ops:
  1.9 12.5 %collective-permute-start = (bf16[1,69632]{1,0:T(2,128)(2,1)S(1)}, bf16[1,69632]{1,0:T(2,128)(2,1)S(1)}, u32[]{:S(2)}, u32[]{:S(2)}) collective-permute-start(bf16[1,69632]{1,0:T(2,128)(2,1)S(1)} %slice.3), channel_id=1, source_target_pairs={{0,31},{1,0},{2,1},{3,2},{4,3},{5,4},{6,5},{7,6},{8,7},{9,8},{10,9... | collective-permute-start | bytes 417800 | tf_op jit(solution)/shard_map/ppermute | solution.py:246
  14.4 0.7 copy-start.1
  475.1 22.3 %copy-start = (bf16[384,1152]{1,0:T(8,128)(2,1)S(1)}, bf16[384,1152]{1,0:T(8,128)(2,1)}, u32[]{:S(2)}) copy-start(bf16[384,1152]{1,0:T(8,128)(2,1)} %get-tuple-element.41) | copy-start | bytes 2654212
  478.6 9.8 %collective-permute-start.1 = (f32[1,69632]{1,0:T(1,128)}, f32[1,69632]{1,0:T(1,128)S(1)}, u32[]{:S(2)}, u32[]{:S(2)}) collective-permute-start(f32[1,69632]{1,0:T(1,128)} %tail.1), channel_id=1, source_target_pairs={{0,1},{1,2},{2,3},{3,4},{4,5},{5,6},{6,7},{7,8},{8,9},{9,10},{10,1... | collective-permute-start | bytes 835592 | tf_op jit(solution)/shard_map/ppermute | solution.py:280
  488.4 0.7 copy-start.2

commit v2 on v1

--- a/solution.py
+++ b/solution.py
@@ -1734,13 +1734,11 @@
         return remote(near_ref.at[slot], near_got.at[which], near_send.at[which], near_recv.at[which], device)
 
 
+    run_ahead([(3, p, 0) for p in late_ids], None)
+
     @pl.loop(0, 4)
     def _(i):
         row_block(jnp.where(i == 0, 0, jnp.where(i == 1, 4, 2 * i - 3)))
-
-        @pl.when(i == 0)
-        def _():
-            run_ahead([(3, p, 0) for p in late_ids], None)
 
         @pl.when(i == 1)
         def _():

time: 500 us -> 498 us (level)
  no operation moved by 1% of the time
where the time goes in v2:
time: 498 us; the launch traced here: 497 us
  Pallas kernels  469 us (94%)
  local copies, waits for them, and re-layouts  12.1 us (2%)
  waiting for transfers between devices  8.5 us (2%)
  starting transfers between devices  6.57 us (1%)
    pallas_call x1, Pallas kernels, back_scatter(): pl.pallas_call(functools.partial(back_scatter_kernel, depth, where, early...  220 us
    pallas_call x1, Pallas kernels, gather_front(): pl.pallas_call(functools.partial(gather_front_kernel, depth, where, early...  173 us
    pallas_call x1, Pallas kernels, middle(): pl.pallas_call(functools.partial(middle_kernel, where), out_shape=(shape(...  56.6 us
    pallas_call x2, Pallas kernels, call(): pl.pallas_call(functools.partial(to_flat_kernel, entries, rows), out_shap...  11.8 us
  transfers between devices with their start and end apart: 2, of which 1 were waited for; matrix products, arithmetic and copies ran while one was open for 1% of the time, Pallas kernels for 0%

profile of v2, /device:TPU:0, one launch (start us, length us, event | category | flops | bytes accessed | tf_op | source)
XLA Modules:
  0.0 496.8 jit_solution(1163652741499604432)
XLA Ops:
  0.6 1.2 slice.3
  1.9 6.5 %collective-permute-start = (bf16[1,69632]{1,0:T(2,128)(2,1)S(1)}, bf16[1,69632]{1,0:T(2,128)(2,1)S(1)}, u32[]{:S(2)}, u32[]{:S(2)}) collective-permute-start(bf16[1,69632]{1,0:T(2,128)(2,1)S(1)} %slice.3), channel_id=1, source_target_pairs={{0,31},{1,0},{2,1},{3,2},{4,3},{5,4},{6,5},{7,6},{8,7},{9,8},{10,9... | collective-permute-start | bytes 417800 | tf_op jit(solution)/shard_map/ppermute | solution.py:246
  8.3 0.8 pad_dynamic-slice_fusion
  9.1 1.3 fusion.table_ref
  10.4 0.8 dynamic_slice.19
  11.2 0.8 broadcast_in_dim.19.segq_ref
  12.0 0.6 broadcast_in_dim.17.segq_ref
  12.5 0.6 broadcast_in_dim.16.segk_ref
  13.1 1.3 fusion.2.table_ref
  14.4 0.0 collective-permute-done.head_ref
  14.4 0.0 copy-start.1
  14.4 0.7 copy-done.1
  15.1 7.8 %to_tiles.1.block_ref = bf16[242,16,128]{2,1,0:T(8,128)(2,1)} custom-call(s32[81]{0:T(128)} %fusion.table_ref, bf16[1,476288]{1,0:T(2,128)(2,1)} %line_ref.1, bf16[1,69632]{1,0:T(2,128)(2,1)} %copy-done.1), custom_call_target="tpu_custom_call" | custom-call | tf_op jit(solution)/shard_map/to_tiles/pallas_call | solution.py:248
  22.9 172.7 %gather_front.1 = (bf16[32,242,16,128]{3,2,1,0:T(8,128)(2,1)}, bf16[1920,1152]{1,0:T(8,128)(2,1)}, bf16[1152,1920]{1,0:T(8,128)(2,1)}, bf16[1152,1920]{1,0:T(8,1...) custom-call(bf16[242,16,128]{2,1,0:T(8,128)(2,1)} %to_tiles.1.block_, ...), custom_call_target="tpu_custom_call" | custom-call | tf_op jit(solution)/shard_map/gather_front/pallas_call | solution.py:1319
  195.6 56.6 %middle.1 = (bf16[384,1152]{1,0:T(8,128)(2,1)}, f32[384,1152]{1,0:T(8,128)}, bf16[384,1152]{1,0:T(8,128)(2,1)}, f32[16,384]{1,0:T(8,128)}, bf16[32,242,16,128]{3,2,1,0:T(8,128)(2,1)}) custom-call(bf16[384,1152]{1,0:T(8,128)(2,1)} %x_ref.1, bf16[384,1152]{1,0:T(8,128)(2,1)} %cot_ref.1, bf16[384,1152]{1,0:T(8,128)(2,1)} %get-tuple-element.20.attended_ref, ...), custom_call_target="tpu_custom_call" | custom-call | tf_op jit(solution)/shard_map/middle/pallas_call | solution.py:640
  252.2 1.3 broadcast_in_dim.18.segk_ref
  253.5 220.1 %back_scatter.1 = (bf16[32,242,16,128]{3,2,1,0:T(8,128)(2,1)}, f32[242,16,128]{2,1,0:T(8,128)}, bf16[384,1152]{1,0:T(8,128)(2,1)}, bf16[4,4,242,16,128]{4,3,2,1,...) custom-call(bf16[1920,1152]{1,0:T(8,128)(2,1)} %get-tuple-element.24, ...), custom_call_target="tpu_custom_call", output_to_operand_aliasing={{0}: (13, {})} | custom-call | tf_op jit(solution)/shard_map/back_scatter/pallas_call | solution.py:1887
  473.5 0.0 copy-start
  473.6 3.5 tail.1
  477.1 0.1 collective-permute-start.1
  477.2 1.2 fusion.1.table_ref
  478.3 8.5 %collective-permute-done.1.refs_0_ = f32[1,69632]{1,0:T(1,128)S(1)} collective-permute-done((f32[1,69632]{1,0:T(1,128)}, f32[1,69632]{1,0:T(1,128)S(1)}, u32[]{:S(2)}, u32[]{:S(2)}) %collective-permute-start.1) | collective-permute-done | bytes 278560 | tf_op jit(solution)/shard_map/ppermute | solution.py:280
  486.8 0.0 copy-start.2
  486.8 0.7 copy-done.2
  487.5 8.3 %to_flat.1 = f32[1,476288]{1,0:T(1,128)} custom-call(s32[82]{0:T(128)} %fusion.1.table_ref, f32[242,16,128]{2,1,0:T(8,128)} %get-tuple-element.36.tile_ref, f32[1,69632]{1,0:T(1,128)} %copy-done.2), custom_call_target="tpu_custom_call" | custom-call | tf_op jit(solution)/shard_map/to_flat/pallas_call | solution.py:269
  495.9 0.0 copy-done
  495.9 0.9 copy.14
Async XLA Ops:
  1.9 12.5 %collective-permute-start = (bf16[1,69632]{1,0:T(2,128)(2,1)S(1)}, bf16[1,69632]{1,0:T(2,128)(2,1)S(1)}, u32[]{:S(2)}, u32[]{:S(2)}) collective-permute-start(bf16[1,69632]{1,0:T(2,128)(2,1)S(1)} %slice.3), channel_id=1, source_target_pairs={{0,31},{1,0},{2,1},{3,2},{4,3},{5,4},{6,5},{7,6},{8,7},{9,8},{10,9... | collective-permute-start | bytes 417800 | tf_op jit(solution)/shard_map/ppermute | solution.py:246
  14.4 0.7 copy-start.1
  473.5 22.3 %copy-start = (bf16[384,1152]{1,0:T(8,128)(2,1)S(1)}, bf16[384,1152]{1,0:T(8,128)(2,1)}, u32[]{:S(2)}) copy-start(bf16[384,1152]{1,0:T(8,128)(2,1)} %get-tuple-element.41) | copy-start | bytes 2654212
  477.1 9.8 %collective-permute-start.1 = (f32[1,69632]{1,0:T(1,128)}, f32[1,69632]{1,0:T(1,128)S(1)}, u32[]{:S(2)}, u32[]{:S(2)}) collective-permute-start(f32[1,69632]{1,0:T(1,128)} %tail.1), channel_id=1, source_target_pairs={{0,1},{1,2},{2,3},{3,4},{4,5},{5,6},{6,7},{7,8},{8,9},{9,10},{10,1... | collective-permute-start | bytes 835592 | tf_op jit(solution)/shard_map/ppermute | solution.py:280
  486.8 0.7 copy-start.2

commit v3 on v2

--- a/solution.py
+++ b/solution.py
@@ -1742,10 +1742,10 @@
 
         @pl.when(i == 1)
         def _():
+            for p in late_ids:
+                run_ahead([(1, p, 0), (2, p, 0)], None)
             at_plane(1, lambda: run([(0, b, 0)], 1))
             at_plane(2, lambda: run([(0, a, 0), (0, c_, 0)], 2))
-            for p in late_ids:
-                run_ahead([(1, p, 0), (2, p, 0)], None)
 
     sides = [near_save(slot) for slot in (0, 4, 1, 3)]
     start(sides)

time: 498 us -> 492 us (0.988)
  Pallas kernels: 469 us -> 463 us
    pallas_call x1, Pallas kernels: 220 us -> 214 us  [back_scatter(): pl.pallas_call(functools.partial(back_scatter_kernel, depth, where, early...]
where the time goes in v3:
time: 492 us; the launch traced here: 491 us
  Pallas kernels  463 us (94%)
  local copies, waits for them, and re-layouts  12.1 us (2%)
  starting transfers between devices  10.9 us (2%)
    pallas_call x1, Pallas kernels, back_scatter(): pl.pallas_call(functools.partial(back_scatter_kernel, depth, where, early...  214 us
    pallas_call x1, Pallas kernels, gather_front(): pl.pallas_call(functools.partial(gather_front_kernel, depth, where, early...  173 us
    pallas_call x1, Pallas kernels, middle(): pl.pallas_call(functools.partial(middle_kernel, where), out_shape=(shape(...  56.6 us
    pallas_call x2, Pallas kernels, call(): pl.pallas_call(functools.partial(to_flat_kernel, entries, rows), out_shap...  11.8 us
  transfers between devices with their start and end apart: 2, of which 1 were waited for; matrix products, arithmetic and copies ran while one was open for 1% of the time, Pallas kernels for 0%

profile of v3, /device:TPU:0, one launch (start us, length us, event | category | flops | bytes accessed | tf_op | source)
XLA Modules:
  0.0 490.6 jit_solution(15381851535908093503)
XLA Ops:
  0.6 1.2 slice.3
  1.9 6.5 %collective-permute-start = (bf16[1,69632]{1,0:T(2,128)(2,1)S(1)}, bf16[1,69632]{1,0:T(2,128)(2,1)S(1)}, u32[]{:S(2)}, u32[]{:S(2)}) collective-permute-start(bf16[1,69632]{1,0:T(2,128)(2,1)S(1)} %slice.3), channel_id=1, source_target_pairs={{0,31},{1,0},{2,1},{3,2},{4,3},{5,4},{6,5},{7,6},{8,7},{9,8},{10,9... | collective-permute-start | bytes 417800 | tf_op jit(solution)/shard_map/ppermute | solution.py:246
  8.3 0.8 pad_dynamic-slice_fusion
  9.1 1.3 fusion.table_ref
  10.4 0.8 dynamic_slice.19
  11.2 0.8 broadcast_in_dim.19.segq_ref
  12.0 0.6 broadcast_in_dim.17.segq_ref
  12.5 0.6 broadcast_in_dim.16.segk_ref
  13.1 1.3 fusion.2.table_ref
  14.4 0.0 collective-permute-done.head_ref
  14.4 0.0 copy-start.1
  14.4 0.7 copy-done.1
  15.1 7.8 %to_tiles.1.block_ref = bf16[242,16,128]{2,1,0:T(8,128)(2,1)} custom-call(s32[81]{0:T(128)} %fusion.table_ref, bf16[1,476288]{1,0:T(2,128)(2,1)} %line_ref.1, bf16[1,69632]{1,0:T(2,128)(2,1)} %copy-done.1), custom_call_target="tpu_custom_call" | custom-call | tf_op jit(solution)/shard_map/to_tiles/pallas_call | solution.py:248
  22.9 172.7 %gather_front.1 = (bf16[32,242,16,128]{3,2,1,0:T(8,128)(2,1)}, bf16[1920,1152]{1,0:T(8,128)(2,1)}, bf16[1152,1920]{1,0:T(8,128)(2,1)}, bf16[1152,1920]{1,0:T(8,1...) custom-call(bf16[242,16,128]{2,1,0:T(8,128)(2,1)} %to_tiles.1.block_, ...), custom_call_target="tpu_custom_call" | custom-call | tf_op jit(solution)/shard_map/gather_front/pallas_call | solution.py:1319
  195.6 56.6 %middle.1 = (bf16[384,1152]{1,0:T(8,128)(2,1)}, f32[384,1152]{1,0:T(8,128)}, bf16[384,1152]{1,0:T(8,128)(2,1)}, f32[16,384]{1,0:T(8,128)}, bf16[32,242,16,128]{3,2,1,0:T(8,128)(2,1)}) custom-call(bf16[384,1152]{1,0:T(8,128)(2,1)} %x_ref.1, bf16[384,1152]{1,0:T(8,128)(2,1)} %cot_ref.1, bf16[384,1152]{1,0:T(8,128)(2,1)} %get-tuple-element.20.attended_ref, ...), custom_call_target="tpu_custom_call" | custom-call | tf_op jit(solution)/shard_map/middle/pallas_call | solution.py:640
  252.2 1.3 broadcast_in_dim.18.segk_ref
  253.5 213.9 %back_scatter.1 = (bf16[32,242,16,128]{3,2,1,0:T(8,128)(2,1)}, f32[242,16,128]{2,1,0:T(8,128)}, bf16[384,1152]{1,0:T(8,128)(2,1)}, bf16[4,4,242,16,128]{4,3,2,1,...) custom-call(bf16[1920,1152]{1,0:T(8,128)(2,1)} %get-tuple-element.24, ...), custom_call_target="tpu_custom_call", output_to_operand_aliasing={{0}: (13, {})} | custom-call | tf_op jit(solution)/shard_map/back_scatter/pallas_call | solution.py:1887
  467.4 0.0 copy-start
  467.4 3.5 tail.1
  470.9 4.5 collective-permute-start.1
  475.4 1.2 fusion.1.table_ref
  476.5 4.2 collective-permute-done.1.refs_0_
  480.7 0.0 copy-start.2
  480.7 0.7 copy-done.2
  481.4 8.3 %to_flat.1 = f32[1,476288]{1,0:T(1,128)} custom-call(s32[82]{0:T(128)} %fusion.1.table_ref, f32[242,16,128]{2,1,0:T(8,128)} %get-tuple-element.36.tile_ref, f32[1,69632]{1,0:T(1,128)} %copy-done.2), custom_call_target="tpu_custom_call" | custom-call | tf_op jit(solution)/shard_map/to_flat/pallas_call | solution.py:269
  489.7 0.0 copy-done
  489.7 0.9 copy.14
Async XLA Ops:
  1.9 12.5 %collective-permute-start = (bf16[1,69632]{1,0:T(2,128)(2,1)S(1)}, bf16[1,69632]{1,0:T(2,128)(2,1)S(1)}, u32[]{:S(2)}, u32[]{:S(2)}) collective-permute-start(bf16[1,69632]{1,0:T(2,128)(2,1)S(1)} %slice.3), channel_id=1, source_target_pairs={{0,31},{1,0},{2,1},{3,2},{4,3},{5,4},{6,5},{7,6},{8,7},{9,8},{10,9... | collective-permute-start | bytes 417800 | tf_op jit(solution)/shard_map/ppermute | solution.py:246
  14.4 0.7 copy-start.1
  467.4 22.3 %copy-start = (bf16[384,1152]{1,0:T(8,128)(2,1)S(1)}, bf16[384,1152]{1,0:T(8,128)(2,1)}, u32[]{:S(2)}) copy-start(bf16[384,1152]{1,0:T(8,128)(2,1)} %get-tuple-element.41) | copy-start | bytes 2654212
  470.9 9.8 %collective-permute-start.1 = (f32[1,69632]{1,0:T(1,128)}, f32[1,69632]{1,0:T(1,128)S(1)}, u32[]{:S(2)}, u32[]{:S(2)}) collective-permute-start(f32[1,69632]{1,0:T(1,128)} %tail.1), channel_id=1, source_target_pairs={{0,1},{1,2},{2,3},{3,4},{4,5},{5,6},{6,7},{7,8},{8,9},{9,10},{10,1... | collective-permute-start | bytes 835592 | tf_op jit(solution)/shard_map/ppermute | solution.py:280
  480.7 0.7 copy-start.2
